TPU v7x, 128 devices: a whole 4x4x4 slice. The times are simulated.
128 devices in a mesh: tm: 2 (over z_lo), grid: 64 (over z_hi, y, x, core).
Axes of the slice: x: 4, y: 4, z: 4 (z_hi: 2, z_lo: 2; z = z_hi * 2 + z_lo), core: 2. Of those that a mesh axis runs over, the one named last changes fastest.
Arguments:
- occupied_green: bfloat16 [2, 1024, 1024], P('tm', 'grid'), may hold values from -0.005859375 to 0.005859375
- empty_green: bfloat16 [2, 1024, 1024], P('tm', 'grid'), may hold values from -0.005859375 to 0.005859375
- basis: bfloat16 [12288, 1024], P('grid'), may hold values from -8 to 8
- time_weights: float32 [2, 2], replicated, may hold values from 0.25 to 1
Outputs:
- polarizability: float32 [2, 1024, 1024], P('tm', 'grid')
All inputs are finite; a program needn't handle non-finite values.
Results may differ from a plain program's by a relative error of at most 0.0012.
Values may be sent and summed in bfloat16 or wider, within the bound.
No kernel may reach another device: no remote copies, remote signals or barrier semaphores. Data moves between devices by JAX's collectives and lax.ppermute only.
A program may use at most 128 MiB of HBM per device.

v0:
```python
import jax
import jax.numpy as jnp
from jax import lax
from jax.experimental import pallas as pl
from jax.experimental.pallas import tpu as pltpu
from jax.sharding import Mesh
from jax.sharding import PartitionSpec as P


NR = 12288
NB = 1024
GRID = ("zh", "y", "x", "core")
BF = jnp.bfloat16
F32 = jnp.float32
ANY = pl.BlockSpec(memory_space=pl.ANY)
MIB = 1024 * 1024


def shift(v, axis, step):
    n = lax.axis_size(axis)
    return lax.ppermute(v, axis, [(i, (i + step) % n) for i in range(n)])


def far_z(v):
    return lax.ppermute(v, ("tm", "zh"), [(0, 3), (3, 0), (1, 2), (2, 1)])


def nt(a, b):
    return lax.dot_general(a, b, (((1,), (1,)), ((), ())), preferred_element_type=F32)


def copy_all(copies):
    for c in copies:
        c.start()
    for c in copies:
        c.wait()


def row_copies(pieces, dst, sems, first):
    out, row = [], 0
    for j, p in enumerate(pieces):
        rows = p.shape[0]
        out.append(pltpu.make_async_copy(p, dst.at[pl.ds(row, rows)], sems.at[first + j]))
        row += rows
    return out


RING = (0, 3, 1, 2)
DEV_ROWS = 192
R_TILE = 512


def assemble_kernel(*refs):
    pieces, out, sems = refs[:-2], refs[-2], refs[-1]
    x, tm = lax.axis_index("x"), lax.axis_index("tm")
    half = DEV_ROWS // 2
    copies = []
    for n, p in enumerate(pieces):
        row = lax.rem(x + S_RING[n], 4) * DEV_ROWS
        if n >= 3:
            row += half * (tm if n == 3 else 1 - tm)
        to = out.at[pl.ds(pl.multiple_of(row, 32), p.shape[0])]
        copies.append(pltpu.make_async_copy(p, to, sems.at[n]))
    copy_all(copies)


def assemble(pieces):
    return pl.pallas_call(
        assemble_kernel,
        out_shape=jax.ShapeDtypeStruct((4 * DEV_ROWS, NB), BF),
        in_specs=[ANY] * len(pieces),
        out_specs=pl.BlockSpec(memory_space=pltpu.VMEM),
        scratch_shapes=[pltpu.SemaphoreType.DMA((len(pieces),))],
        compiler_params=pltpu.CompilerParams(vmem_limit_bytes=6 * MIB),
        cost_estimate=pl.CostEstimate(flops=10**9, bytes_accessed=6 * MIB, transcendentals=0),
        name="assemble",
    )(*pieces)


def main_kernel(n_r, *refs):
    n_c = 2 * len(RING)
    chunks = refs[:n_c]
    pieces = refs[n_c : n_c + n_r]
    outs = refs[n_c + n_r : n_c + n_r + 4]
    proj, block, block_t, product, r_sems, p_sems = refs[n_c + n_r + 4 :]
    x, core = lax.axis_index("x"), lax.axis_index("core")
    r_rows = block.shape[0]
    s_rows = proj.shape[-1]
    r_copies = row_copies(pieces, block, r_sems, 0)
    p_copies = []
    for n, ref in enumerate(chunks):
        cc = core if n < len(RING) else 1 - core
        xc = lax.rem(x + RING[n % 4], 4) * 2 + cc
        for q in range(2):
            p_copies.append(
                pltpu.make_async_copy(ref.at[q], proj.at[q, :, xc], p_sems.at[2 * n + q])
            )
    for c in p_copies + r_copies:
        c.start()
    for c in p_copies:
        c.wait()

    def real_space(i, carry):
        at = pl.ds(pl.multiple_of(i * R_TILE, R_TILE), R_TILE)
        rows = block[at]
        occupied = jnp.dot(rows, proj[0].reshape(NB, s_rows), preferred_element_type=F32)
        empty = jnp.dot(rows, proj[1].reshape(NB, s_rows), preferred_element_type=F32)
        product[at] = (occupied * empty).astype(BF)
        block_t[:, :, :, at] = rows.T.reshape(8, 4, 32, R_TILE)
        return carry

    tiles = r_rows // R_TILE
    for part in range(2):
        for c in r_copies[part * n_r // 2 : (part + 1) * n_r // 2]:
            c.wait()
        lax.fori_loop(part * tiles // 2, (part + 1) * tiles // 2, real_space, 0)
    for k in range(4):
        rows = block_t[:, lax.rem(x + k, 4)].reshape(NB // 4, r_rows)
        back = jnp.dot(rows, product[...], preferred_element_type=F32).astype(BF)
        outs[k][...] = back.reshape(8, 32, s_rows)


def main(chunks, pieces, s_rows):
    r_rows = sum(p.shape[0] for p in pieces)

    def kernel(*refs):
        main_kernel(len(pieces), *refs)

    return pl.pallas_call(
        kernel,
        out_shape=[jax.ShapeDtypeStruct((8, 32, s_rows), BF)] * 4,
        in_specs=[ANY] * (len(chunks) + len(pieces)),
        out_specs=[pl.BlockSpec(memory_space=pltpu.VMEM)] * 4,
        scratch_shapes=[
            pltpu.VMEM((2, 8, 8, 16, s_rows), BF),
            pltpu.VMEM((r_rows, NB), BF),
            pltpu.VMEM((8, 4, 32, r_rows), BF),
            pltpu.VMEM((r_rows, s_rows), BF),
            pltpu.SemaphoreType.DMA((len(pieces),)),
            pltpu.SemaphoreType.DMA((2 * len(chunks),)),
        ],
        compiler_params=pltpu.CompilerParams(vmem_limit_bytes=32 * MIB),
        cost_estimate=pl.CostEstimate(
            flops=6 * s_rows * r_rows * NB, bytes_accessed=12 * MIB, transcendentals=0
        ),
        name="main",
    )(*chunks, *pieces)


def gather_x(v):
    return [v, shift(v, "x", 1), shift(v, "x", -1), shift(v, "x", 2)]


def both_cores(parts):
    return parts + [shift(v, "core", 1) for v in parts]


S_RING = (0, 3, 1, 2, 2)


def gather_points_x(b):
    half = DEV_ROWS // 2
    part = lax.dynamic_slice_in_dim(b, lax.axis_index("tm") * half, half, 0)
    xm, xp, far = shift(b, "x", 1), shift(b, "x", -1), shift(part, "x", 2)
    return [b, xm, xp, far, shift(far, "tm", 1)]


def gather_points_yz(b):
    zb = far_z(b)
    ym, yp, far = shift(b, "y", 1), shift(b, "y", -1), shift(b, "y", 2)
    zm = far_z(ym)
    zfar = far_z(far)
    zp = shift(zb, "y", -1)
    return [b, ym, yp, far, zb, zp, zm, zfar]


def gather_green_yz(g):
    zh, y = lax.axis_index("zh"), lax.axis_index("y")
    gz = shift(g, "zh", 1)
    first = zh == 0
    pair = jnp.stack([jnp.where(first, g, gz), jnp.where(first, gz, g)], axis=1)
    parts = [pair, shift(pair, "y", -1), shift(pair, "y", 2), shift(pair, "y", 1)]
    out = jnp.zeros((2, 2, 4, 16, NB), BF)
    for k, v in enumerate(parts):
        out = lax.dynamic_update_slice_in_dim(out, v[:, :, None], lax.rem(y + k, 4), 2)
    return out.reshape(2, 8, 16, NB)


def project(green, s_block):
    rows = nt(green.reshape(-1, NB), s_block).astype(BF)
    return rows.reshape(*green.shape[:-1], s_block.shape[0])


def sum_over_x(parts):
    back = parts[0].astype(F32)
    for k in (2, 1, 3):
        back = back + shift(parts[k], "x", k).astype(F32)
    return back.astype(BF).reshape(256, -1)


def reduce_out(coef, time_weights):
    zh, y, core = (lax.axis_index(a) for a in ("zh", "y", "core"))
    tm = lax.axis_index("tm")
    coef = coef.reshape(8, 2, 16, NB)

    def for_core(k):
        return lax.dynamic_index_in_dim(coef, k, 1, keepdims=False)

    coef = for_core(core) + shift(for_core(1 - core), "core", 1)
    coef = coef.reshape(2, 4, 16, NB)

    def for_y(k):
        return lax.dynamic_index_in_dim(coef, lax.rem(y + k, 4), 1, keepdims=False)

    col = for_y(0)
    for k in (1, 3, 2):
        col = col + shift(for_y(k), "y", k)

    def weighted(f, z):
        w = lax.dynamic_slice(time_weights, (f, tm), (1, 1)) * (1.0 / NR)
        return w * lax.dynamic_index_in_dim(col, z, 0, keepdims=False)

    out = weighted(tm, zh)
    out = out + shift(weighted(1 - tm, zh), "tm", 1)
    out = out + shift(weighted(tm, 1 - zh), "zh", 1)
    out = out + far_z(weighted(1 - tm, 1 - zh))
    return out[None]


def shards(occupied_green, empty_green, basis, time_weights):
    green = jnp.stack([occupied_green[0], empty_green[0]])
    green = gather_green_yz(green)
    s_pieces = gather_points_x(basis)
    s_block = assemble(s_pieces)
    r_pieces = both_cores(gather_points_yz(basis))
    greens = both_cores(gather_x(green))
    chunks = [project(v, s_block) for v in greens]
    parts = main(chunks, r_pieces, s_block.shape[0])
    coef = jnp.dot(sum_over_x(parts), s_block, preferred_element_type=F32)
    return reduce_out(coef, time_weights)


def solution(mesh):
    split = Mesh(
        mesh.devices.reshape(mesh.shape["tm"], 2, 4, 4, 2),
        ("tm", "zh", "y", "x", "core"),
    )
    in_specs = (P("tm", GRID, None), P("tm", GRID, None), P(GRID, None), P())
    out_specs = P("tm", GRID, None)

    return jax.shard_map(
        shards, mesh=split, in_specs=in_specs, out_specs=out_specs, check_vma=False
    )
```

profile of v0, /device:TPU:0, one launch (start us, length us, event | category | flops | bytes accessed | tf_op | source)
XLA Modules:
  0.0 156.7 jit_solution(634382452556994428)
XLA Ops:
  0.0 0.8 constant_dynamic-update-slice_fusion.1
  0.8 0.8 constant_dynamic-update-slice_fusion
  1.6 4.0 %collective-permute-start = (bf16[2,16,1024]{2,1,0:T(8,128)(2,1)S(1)}, bf16[2,16,1024]{2,1,0:T(8,128)(2,1)S(1)}, u32[]{:S(2)}, u32[]{:S(2)}) collective-permute-start(bf16[2,16,1024]{2,1,0:T(8,128)(2,1)S(1)} %constant_dynamic-update-slice_fusion), channel_id=1, source_target_pairs={{0,32},{32,0},{1,33},{33,1},{2,34},{34,2},{3,35},{35,3},{4,36},{36... | collective-permute-start | bytes 196616 | tf_op jit(solution)/shard_map/ppermute | solution.py:21
  5.6 2.2 %collective-permute-done = bf16[2,16,1024]{2,1,0:T(8,128)(2,1)S(1)} collective-permute-done((bf16[2,16,1024]{2,1,0:T(8,128)(2,1)S(1)}, bf16[2,16,1024]{2,1,0:T(8,128)(2,1)S(1)}, u32[]{:S(2)}, u32[]{:S(2)}) %collective-permute-start) | collective-permute-done | bytes 65568 | tf_op jit(solution)/shard_map/ppermute | solution.py:21
  7.8 3.1 %collective-permute-start.1 = (bf16[2,2,16,1024]{3,2,1,0:T(8,128)(2,1)S(1)}, bf16[2,2,16,1024]{3,2,1,0:T(8,128)(2,1)S(1)}, u32[]{:S(2)}, u32[]{:S(2)}) collective-permute-start(bf16[2,2,16,1024]{3,2,1,0:T(8,128)(2,1)S(1)} %pad_maximum_fusion), channel_id=1, source_target_pairs={{0,24},{8,0},{16,8},{24,16},{1,25},{9,1},{17,9},{25,17},{2,26},{10... | collective-permute-start | bytes 393224 | tf_op jit(solution)/shard_map/ppermute | solution.py:21
  10.9 0.6 collective-permute-start.2
  11.6 1.0 collective-permute-start.3
  12.6 3.0 %collective-permute-done.1 = bf16[2,2,16,1024]{3,2,1,0:T(8,128)(2,1)S(1)} collective-permute-done((bf16[2,2,16,1024]{3,2,1,0:T(8,128)(2,1)S(1)}, bf16[2,2,16,1024]{3,2,1,0:T(8,128)(2,1)S(1)}, u32[]{:S(2)}, u32[]{:S(2)}) %collective-permute-start.1) | collective-permute-done | bytes 131104 | tf_op jit(solution)/shard_map/ppermute | solution.py:21
  15.7 2.3 %collective-permute-done.2 = bf16[2,2,16,1024]{3,2,1,0:T(8,128)(2,1)S(1)} collective-permute-done((bf16[2,2,16,1024]{3,2,1,0:T(8,128)(2,1)S(1)}, bf16[2,2,16,1024]{3,2,1,0:T(8,128)(2,1)S(1)}, u32[]{:S(2)}, u32[]{:S(2)}) %collective-permute-start.2) | collective-permute-done | bytes 131104 | tf_op jit(solution)/shard_map/ppermute | solution.py:21
  17.9 1.4 collective-permute-done.3
  19.3 2.8 %collective-permute-start.9 = (bf16[2,8,16,1024]{3,2,1,0:T(8,128)(2,1)S(1)}, bf16[2,8,16,1024]{3,2,1,0:T(8,128)(2,1)S(1)}, u32[]{:S(2)}, u32[]{:S(2)}) collective-permute-start(bf16[2,8,16,1024]{3,2,1,0:T(8,128)(2,1)S(1)} %bitcast.105), channel_id=1, source_target_pairs={{0,6},{2,0},{4,2},{6,4},{1,7},{3,1},{5,3},{7,5},{8,14},{10,8},{12,... | collective-permute-start | bytes 1572872 | tf_op jit(solution)/shard_map/ppermute | solution.py:21
  22.2 0.9 collective-permute-start.6
  23.1 0.9 collective-permute-start.4
  24.0 2.4 %collective-permute-start.5 = (bf16[192,1024]{1,0:T(8,128)(2,1)S(1)}, bf16[192,1024]{1,0:T(8,128)(2,1)S(1)}, u32[]{:S(2)}, u32[]{:S(2)}) collective-permute-start(bf16[192,1024]{1,0:T(8,128)(2,1)S(1)} %copy-done), channel_id=1, source_target_pairs={{0,6},{2,0},{4,2},{6,4},{1,7},{3,1},{5,3},{7,5},{8,14},{10,8},{12,... | collective-permute-start | bytes 1179656 | tf_op jit(solution)/shard_map/ppermute | solution.py:21
  26.3 3.4 %collective-permute-start.18 = (bf16[192,1024]{1,0:T(8,128)(2,1)S(1)}, bf16[192,1024]{1,0:T(8,128)(2,1)S(1)}, u32[]{:S(2)}, u32[]{:S(2)}) collective-permute-start(bf16[192,1024]{1,0:T(8,128)(2,1)S(1)} %copy-done), channel_id=1, source_target_pairs={{0,96},{96,0},{32,64},{64,32},{1,97},{97,1},{33,65},{65,33},{2,98}... | collective-permute-start | bytes 1179656 | tf_op jit(solution)/shard_map/ppermute | solution.py:25
  29.7 1.8 %collective-permute-done.6.refs_3_ = bf16[96,1024]{1,0:T(8,128)(2,1)S(1)} collective-permute-done((bf16[96,1024]{1,0:T(8,128)(2,1)S(1)}, bf16[96,1024]{1,0:T(8,128)(2,1)S(1)}, u32[]{:S(2)}, u32[]{:S(2)}) %collective-permute-start.6) | collective-permute-done | bytes 196640 | tf_op jit(solution)/shard_map/ppermute | solution.py:21
  31.6 1.3 collective-permute-start.7
  32.8 4.4 %collective-permute-done.7.refs_4_ = bf16[96,1024]{1,0:T(8,128)(2,1)S(1)} collective-permute-done((bf16[96,1024]{1,0:T(8,128)(2,1)S(1)}, bf16[96,1024]{1,0:T(8,128)(2,1)S(1)}, u32[]{:S(2)}, u32[]{:S(2)}) %collective-permute-start.7) | collective-permute-done | bytes 196640 | tf_op jit(solution)/shard_map/ppermute | solution.py:21
  37.2 0.6 collective-permute-done.4.refs_1_
  37.8 1.5 collective-permute-start.17
  39.3 6.0 %collective-permute-done.5.refs_2_ = bf16[192,1024]{1,0:T(8,128)(2,1)S(1)} collective-permute-done((bf16[192,1024]{1,0:T(8,128)(2,1)S(1)}, bf16[192,1024]{1,0:T(8,128)(2,1)S(1)}, u32[]{:S(2)}, u32[]{:S(2)}) %collective-permute-start.5) | collective-permute-done | bytes 393248 | tf_op jit(solution)/shard_map/ppermute | solution.py:21
  45.2 3.3 %collective-permute-start.8 = (bf16[2,8,16,1024]{3,2,1,0:T(8,128)(2,1)S(1)}, bf16[2,8,16,1024]{3,2,1,0:T(8,128)(2,1)S(1)}, u32[]{:S(2)}, u32[]{:S(2)}) collective-permute-start(bf16[2,8,16,1024]{3,2,1,0:T(8,128)(2,1)S(1)} %bitcast.106), channel_id=1, source_target_pairs={{0,2},{2,4},{4,6},{6,0},{1,3},{3,5},{5,7},{7,1},{8,10},{10,12},{12... | collective-permute-start | bytes 1572872 | tf_op jit(solution)/shard_map/ppermute | solution.py:21
  48.6 1.1 assemble.1
  49.7 1.9 %collective-permute-start.10 = (bf16[2,8,16,1024]{3,2,1,0:T(8,128)(2,1)S(1)}, bf16[2,8,16,1024]{3,2,1,0:T(8,128)(2,1)S(1)}, u32[]{:S(2)}, u32[]{:S(2)}) collective-permute-start(bf16[2,8,16,1024]{3,2,1,0:T(8,128)(2,1)S(1)} %bitcast.107), channel_id=1, source_target_pairs={{0,4},{2,6},{4,0},{6,2},{1,5},{3,7},{5,1},{7,3},{8,12},{10,14},{12... | collective-permute-start | bytes 1572872 | tf_op jit(solution)/shard_map/ppermute | solution.py:21
  51.6 0.6 convolution_convert_fusion.7
  52.2 0.6 convolution_convert_fusion.5
  52.8 1.6 %collective-permute-done.15.refs_9_ = bf16[192,1024]{1,0:T(8,128)(2,1)S(1)} collective-permute-done((bf16[192,1024]{1,0:T(8,128)(2,1)S(1)}, bf16[192,1024]{1,0:T(8,128)(2,1)S(1)}, u32[]{:S(2)}, u32[]{:S(2)}) %collective-permute-start.15) | collective-permute-done | bytes 393248 | tf_op jit(solution)/shard_map/ppermute | solution.py:21
  54.5 6.4 %collective-permute-done.8 = bf16[2,8,16,1024]{3,2,1,0:T(8,128)(2,1)S(1)} collective-permute-done((bf16[2,8,16,1024]{3,2,1,0:T(8,128)(2,1)S(1)}, bf16[2,8,16,1024]{3,2,1,0:T(8,128)(2,1)S(1)}, u32[]{:S(2)}, u32[]{:S(2)}) %collective-permute-start.8) | collective-permute-done | bytes 524320 | tf_op jit(solution)/shard_map/ppermute | solution.py:21
  60.9 1.1 collective-permute-start.19
  62.0 9.7 %collective-permute-done.10 = bf16[2,8,16,1024]{3,2,1,0:T(8,128)(2,1)S(1)} collective-permute-done((bf16[2,8,16,1024]{3,2,1,0:T(8,128)(2,1)S(1)}, bf16[2,8,16,1024]{3,2,1,0:T(8,128)(2,1)S(1)}, u32[]{:S(2)}, u32[]{:S(2)}) %collective-permute-start.10) | collective-permute-done | bytes 524320 | tf_op jit(solution)/shard_map/ppermute | solution.py:21
  71.6 0.5 collective-permute-start.20
  72.2 0.6 convolution_convert_fusion.4
  72.8 0.6 convolution_convert_fusion.3
  73.5 0.6 collective-permute-start.23
  74.0 2.7 %collective-permute-start.21 = (bf16[192,1024]{1,0:T(8,128)(2,1)S(1)}, bf16[192,1024]{1,0:T(8,128)(2,1)S(1)}, u32[]{:S(2)}, u32[]{:S(2)}) collective-permute-start(bf16[192,1024]{1,0:T(8,128)(2,1)S(1)} %collective-permute-done.17.refs_11_), channel_id=1, source_target_pairs={{0,96},{96,0},{32,64},{64,32},{1,97},{97,1},{33,65},{65,33},{2,98}... | collective-permute-start | bytes 1179656 | tf_op jit(solution)/shard_map/ppermute | solution.py:25
  76.7 7.7 %collective-permute-done.20.refs_14_ = bf16[192,1024]{1,0:T(8,128)(2,1)S(1)} collective-permute-done((bf16[192,1024]{1,0:T(8,128)(2,1)S(1)}, bf16[192,1024]{1,0:T(8,128)(2,1)S(1)}, u32[]{:S(2)}, u32[]{:S(2)}) %collective-permute-start.20) | collective-permute-done | bytes 393248 | tf_op jit(solution)/shard_map/ppermute | solution.py:25
  84.5 0.5 collective-permute-start.14
  85.0 0.6 convolution_convert_fusion.6
  85.6 0.6 convolution_convert_fusion.2
  86.3 3.4 %collective-permute-done.21.refs_15_ = bf16[192,1024]{1,0:T(8,128)(2,1)S(1)} collective-permute-done((bf16[192,1024]{1,0:T(8,128)(2,1)S(1)}, bf16[192,1024]{1,0:T(8,128)(2,1)S(1)}, u32[]{:S(2)}, u32[]{:S(2)}) %collective-permute-start.21) | collective-permute-done | bytes 393248 | tf_op jit(solution)/shard_map/ppermute | solution.py:25
  89.7 0.5 collective-permute-start.24
  90.2 0.3 collective-permute-start.27
  90.7 0.3 collective-permute-start.29
  90.9 0.6 convolution_convert_fusion.1
  91.6 0.6 convolution_convert_fusion
  92.5 0.6 collective-permute-done.28.refs_22_
  93.1 0.6 collective-permute-done.29.refs_23_
  93.6 20.1 %main.1 = (bf16[8,32,768]{2,1,0:T(8,128)(2,1)S(1)}, bf16[8,32,768]{2,1,0:T(8,128)(2,1)S(1)}, bf16[8,32,768]{2,1,0:T(8,128)(2,1)S(1)}, bf16[8,32,768]{2,1,0:T(8,128)(2,1)S(1)}) custom-call(bf16[2,8,16,768]{3,2,1,0:T(8,128)(2,1)S(1)} %bitcast.95, bf16[2,8,16,768]{3,2,1,0:T(8,128)(2,1)S(1)} %bitcast.99, bf16[2,8,16,768]{3,2,1,0:T(8,128)(2,1)S(1)} %bitcast.96, ...), custom_call_target="tpu_custom_call" | custom-call | flops 14495514624 | bytes 12582912 | tf_op jit(solution)/shard_map/main/pallas_call | solution.py:129
  113.9 3.2 %collective-permute-start.32 = (bf16[8,32,768]{2,1,0:T(8,128)(2,1)S(1)}, bf16[8,32,768]{2,1,0:T(8,128)(2,1)}, u32[]{:S(2)}, u32[]{:S(2)}) collective-permute-start(bf16[8,32,768]{2,1,0:T(8,128)(2,1)S(1)} %get-tuple-element.12), channel_id=1, source_target_pairs={{0,6},{2,0},{4,2},{6,4},{1,7},{3,1},{5,3},{7,5},{8,14},{10,8},{12,... | collective-permute-start | bytes 1179656 | tf_op jit(solution)/shard_map/ppermute | solution.py:21
  117.1 10.2 %collective-permute-done.30 = bf16[8,32,768]{2,1,0:T(8,128)(2,1)S(1)} collective-permute-done((bf16[8,32,768]{2,1,0:T(8,128)(2,1)S(1)}, bf16[8,32,768]{2,1,0:T(8,128)(2,1)S(1)}, u32[]{:S(2)}, u32[]{:S(2)}) %collective-permute-start.30) | collective-permute-done | bytes 393248 | tf_op jit(solution)/shard_map/ppermute | solution.py:21
  127.3 7.4 %collective-permute-done.31 = bf16[8,32,768]{2,1,0:T(8,128)(2,1)} collective-permute-done((bf16[8,32,768]{2,1,0:T(8,128)(2,1)S(1)}, bf16[8,32,768]{2,1,0:T(8,128)(2,1)}, u32[]{:S(2)}, u32[]{:S(2)}) %collective-permute-start.31) | collective-permute-done | bytes 393248 | tf_op jit(solution)/shard_map/ppermute | solution.py:21
  134.8 1.3 add_convert_fusion
  136.1 0.6 fusion
  136.8 1.9 %collective-permute-done.33 = f32[8,16,1024]{2,1,0:T(8,128)S(1)} collective-permute-done((f32[8,16,1024]{2,1,0:T(8,128)S(1)}, f32[8,16,1024]{2,1,0:T(8,128)S(1)}, u32[]{:S(2)}, u32[]{:S(2)}) %collective-permute-start.33) | collective-permute-done | bytes 524320 | tf_op jit(solution)/shard_map/ppermute | solution.py:21
  138.9 3.2 %collective-permute-start.35 = (f32[2,16,1024]{2,1,0:T(8,128)S(1)}, f32[2,16,1024]{2,1,0:T(8,128)S(1)}, u32[]{:S(2)}, u32[]{:S(2)}) collective-permute-start(f32[2,16,1024]{2,1,0:T(8,128)S(1)} %get-tuple-element.15), channel_id=1, source_target_pairs={{0,24},{8,0},{16,8},{24,16},{1,25},{9,1},{17,9},{25,17},{2,26},{10... | collective-permute-start | bytes 393224 | tf_op jit(solution)/shard_map/ppermute | solution.py:21
  142.2 0.6 fusion.7
  144.0 1.7 %collective-permute-done.34 = f32[2,16,1024]{2,1,0:T(8,128)S(1)} collective-permute-done((f32[2,16,1024]{2,1,0:T(8,128)S(1)}, f32[2,16,1024]{2,1,0:T(8,128)S(1)}, u32[]{:S(2)}, u32[]{:S(2)}) %collective-permute-start.34) | collective-permute-done | bytes 131104 | tf_op jit(solution)/shard_map/ppermute | solution.py:21
  145.7 2.1 %collective-permute-done.35 = f32[2,16,1024]{2,1,0:T(8,128)S(1)} collective-permute-done((f32[2,16,1024]{2,1,0:T(8,128)S(1)}, f32[2,16,1024]{2,1,0:T(8,128)S(1)}, u32[]{:S(2)}, u32[]{:S(2)}) %collective-permute-start.35) | collective-permute-done | bytes 131104 | tf_op jit(solution)/shard_map/ppermute | solution.py:21
  147.8 0.9 collective-permute-done.36
  148.8 1.7 %collective-permute-start.38 = (f32[16,1024]{1,0:T(8,128)S(1)}, f32[16,1024]{1,0:T(8,128)S(1)}, u32[]{:S(2)}, u32[]{:S(2)}) collective-permute-start(f32[16,1024]{1,0:T(8,128)S(1)} %get-tuple-element.18), channel_id=1, source_target_pairs={{0,32},{32,0},{1,33},{33,1},{2,34},{34,2},{3,35},{35,3},{4,36},{36... | collective-permute-start | bytes 196616 | tf_op jit(solution)/shard_map/ppermute | solution.py:21
  150.6 3.0 %collective-permute-start.39 = (f32[16,1024]{1,0:T(8,128)S(1)}, f32[16,1024]{1,0:T(8,128)S(1)}, u32[]{:S(2)}, u32[]{:S(2)}) collective-permute-start(f32[16,1024]{1,0:T(8,128)S(1)} %get-tuple-element.17), channel_id=1, source_target_pairs={{0,96},{96,0},{32,64},{64,32},{1,97},{97,1},{33,65},{65,33},{2,98}... | collective-permute-start | bytes 196616 | tf_op jit(solution)/shard_map/ppermute | solution.py:25
  153.5 1.2 collective-permute-done.38
  154.7 1.4 collective-permute-done.39
  156.0 0.6 fusion.6
  (49 shorter events, 1.3 us)
Async XLA Ops:
  0.0 22.2 %copy-start = (bf16[192,1024]{1,0:T(8,128)(2,1)S(1)}, bf16[192,1024]{1,0:T(8,128)(2,1)}, u32[]{:S(2)}) copy-start(bf16[192,1024]{1,0:T(8,128)(2,1)} %refs_8_.1) | copy-start | bytes 1179652
  1.6 6.2 %collective-permute-start = (bf16[2,16,1024]{2,1,0:T(8,128)(2,1)S(1)}, bf16[2,16,1024]{2,1,0:T(8,128)(2,1)S(1)}, u32[]{:S(2)}, u32[]{:S(2)}) collective-permute-start(bf16[2,16,1024]{2,1,0:T(8,128)(2,1)S(1)} %constant_dynamic-update-slice_fusion), channel_id=1, source_target_pairs={{0,32},{32,0},{1,33},{33,1},{2,34},{34,2},{3,35},{35,3},{4,36},{36... | collective-permute-start | bytes 196616 | tf_op jit(solution)/shard_map/ppermute | solution.py:21
  7.8 7.8 %collective-permute-start.1 = (bf16[2,2,16,1024]{3,2,1,0:T(8,128)(2,1)S(1)}, bf16[2,2,16,1024]{3,2,1,0:T(8,128)(2,1)S(1)}, u32[]{:S(2)}, u32[]{:S(2)}) collective-permute-start(bf16[2,2,16,1024]{3,2,1,0:T(8,128)(2,1)S(1)} %pad_maximum_fusion), channel_id=1, source_target_pairs={{0,24},{8,0},{16,8},{24,16},{1,25},{9,1},{17,9},{25,17},{2,26},{10... | collective-permute-start | bytes 393224 | tf_op jit(solution)/shard_map/ppermute | solution.py:21
  10.9 7.0 %collective-permute-start.2 = (bf16[2,2,16,1024]{3,2,1,0:T(8,128)(2,1)S(1)}, bf16[2,2,16,1024]{3,2,1,0:T(8,128)(2,1)S(1)}, u32[]{:S(2)}, u32[]{:S(2)}) collective-permute-start(bf16[2,2,16,1024]{3,2,1,0:T(8,128)(2,1)S(1)} %pad_maximum_fusion), channel_id=1, source_target_pairs={{0,16},{8,24},{16,0},{24,8},{1,17},{9,25},{17,1},{25,9},{2,18},{10... | collective-permute-start | bytes 393224 | tf_op jit(solution)/shard_map/ppermute | solution.py:21
  11.6 7.8 %collective-permute-start.3 = (bf16[2,2,16,1024]{3,2,1,0:T(8,128)(2,1)S(1)}, bf16[2,2,16,1024]{3,2,1,0:T(8,128)(2,1)S(1)}, u32[]{:S(2)}, u32[]{:S(2)}) collective-permute-start(bf16[2,2,16,1024]{3,2,1,0:T(8,128)(2,1)S(1)} %pad_maximum_fusion), channel_id=1, source_target_pairs={{0,8},{8,16},{16,24},{24,0},{1,9},{9,17},{17,25},{25,1},{2,10},{10... | collective-permute-start | bytes 393224 | tf_op jit(solution)/shard_map/ppermute | solution.py:21
  19.3 32.3 %collective-permute-start.9 = (bf16[2,8,16,1024]{3,2,1,0:T(8,128)(2,1)S(1)}, bf16[2,8,16,1024]{3,2,1,0:T(8,128)(2,1)S(1)}, u32[]{:S(2)}, u32[]{:S(2)}) collective-permute-start(bf16[2,8,16,1024]{3,2,1,0:T(8,128)(2,1)S(1)} %bitcast.105), channel_id=1, source_target_pairs={{0,6},{2,0},{4,2},{6,4},{1,7},{3,1},{5,3},{7,5},{8,14},{10,8},{12,... | collective-permute-start | bytes 1572872 | tf_op jit(solution)/shard_map/ppermute | solution.py:21
  22.2 9.4 %collective-permute-start.6 = (bf16[96,1024]{1,0:T(8,128)(2,1)S(1)}, bf16[96,1024]{1,0:T(8,128)(2,1)S(1)}, u32[]{:S(2)}, u32[]{:S(2)}) collective-permute-start(bf16[96,1024]{1,0:T(8,128)(2,1)S(1)} %constant_dynamic-slice_fusion), channel_id=1, source_target_pairs={{0,4},{2,6},{4,0},{6,2},{1,5},{3,7},{5,1},{7,3},{8,12},{10,14},{12... | collective-permute-start | bytes 589832 | tf_op jit(solution)/shard_map/ppermute | solution.py:21
  23.1 14.7 %collective-permute-start.4 = (bf16[192,1024]{1,0:T(8,128)(2,1)S(1)}, bf16[192,1024]{1,0:T(8,128)(2,1)S(1)}, u32[]{:S(2)}, u32[]{:S(2)}) collective-permute-start(bf16[192,1024]{1,0:T(8,128)(2,1)S(1)} %copy-done), channel_id=1, source_target_pairs={{0,2},{2,4},{4,6},{6,0},{1,3},{3,5},{5,7},{7,1},{8,10},{10,12},{12... | collective-permute-start | bytes 1179656 | tf_op jit(solution)/shard_map/ppermute | solution.py:21
  24.0 21.3 %collective-permute-start.5 = (bf16[192,1024]{1,0:T(8,128)(2,1)S(1)}, bf16[192,1024]{1,0:T(8,128)(2,1)S(1)}, u32[]{:S(2)}, u32[]{:S(2)}) collective-permute-start(bf16[192,1024]{1,0:T(8,128)(2,1)S(1)} %copy-done), channel_id=1, source_target_pairs={{0,6},{2,0},{4,2},{6,4},{1,7},{3,1},{5,3},{7,5},{8,14},{10,8},{12,... | collective-permute-start | bytes 1179656 | tf_op jit(solution)/shard_map/ppermute | solution.py:21
  26.3 23.4 %collective-permute-start.18 = (bf16[192,1024]{1,0:T(8,128)(2,1)S(1)}, bf16[192,1024]{1,0:T(8,128)(2,1)S(1)}, u32[]{:S(2)}, u32[]{:S(2)}) collective-permute-start(bf16[192,1024]{1,0:T(8,128)(2,1)S(1)} %copy-done), channel_id=1, source_target_pairs={{0,96},{96,0},{32,64},{64,32},{1,97},{97,1},{33,65},{65,33},{2,98}... | collective-permute-start | bytes 1179656 | tf_op jit(solution)/shard_map/ppermute | solution.py:25
  31.6 5.7 %collective-permute-start.7 = (bf16[96,1024]{1,0:T(8,128)(2,1)S(1)}, bf16[96,1024]{1,0:T(8,128)(2,1)S(1)}, u32[]{:S(2)}, u32[]{:S(2)}) collective-permute-start(bf16[96,1024]{1,0:T(8,128)(2,1)S(1)} %collective-permute-done.6.refs_3_), channel_id=1, source_target_pairs={{0,64},{64,0},{1,65},{65,1},{2,66},{66,2},{3,67},{67,3},{4,68},{68... | collective-permute-start | bytes 589832 | tf_op jit(solution)/shard_map/ppermute | solution.py:21
  37.2 17.3 %collective-permute-start.15 = (bf16[192,1024]{1,0:T(8,128)(2,1)S(1)}, bf16[192,1024]{1,0:T(8,128)(2,1)S(1)}, u32[]{:S(2)}, u32[]{:S(2)}) collective-permute-start(bf16[192,1024]{1,0:T(8,128)(2,1)S(1)} %copy-done), channel_id=1, source_target_pairs={{0,8},{8,16},{16,24},{24,0},{1,9},{9,17},{17,25},{25,1},{2,10},{10... | collective-permute-start | bytes 1179656 | tf_op jit(solution)/shard_map/ppermute | solution.py:21
  37.8 16.7 %collective-permute-start.17 = (bf16[192,1024]{1,0:T(8,128)(2,1)S(1)}, bf16[192,1024]{1,0:T(8,128)(2,1)S(1)}, u32[]{:S(2)}, u32[]{:S(2)}) collective-permute-start(bf16[192,1024]{1,0:T(8,128)(2,1)S(1)} %copy-done), channel_id=1, source_target_pairs={{0,16},{8,24},{16,0},{24,8},{1,17},{9,25},{17,1},{25,9},{2,18},{10... | collective-permute-start | bytes 1179656 | tf_op jit(solution)/shard_map/ppermute | solution.py:21
  45.2 15.6 %collective-permute-start.8 = (bf16[2,8,16,1024]{3,2,1,0:T(8,128)(2,1)S(1)}, bf16[2,8,16,1024]{3,2,1,0:T(8,128)(2,1)S(1)}, u32[]{:S(2)}, u32[]{:S(2)}) collective-permute-start(bf16[2,8,16,1024]{3,2,1,0:T(8,128)(2,1)S(1)} %bitcast.106), channel_id=1, source_target_pairs={{0,2},{2,4},{4,6},{6,0},{1,3},{3,5},{5,7},{7,1},{8,10},{10,12},{12... | collective-permute-start | bytes 1572872 | tf_op jit(solution)/shard_map/ppermute | solution.py:21
  49.7 21.9 %collective-permute-start.10 = (bf16[2,8,16,1024]{3,2,1,0:T(8,128)(2,1)S(1)}, bf16[2,8,16,1024]{3,2,1,0:T(8,128)(2,1)S(1)}, u32[]{:S(2)}, u32[]{:S(2)}) collective-permute-start(bf16[2,8,16,1024]{3,2,1,0:T(8,128)(2,1)S(1)} %bitcast.107), channel_id=1, source_target_pairs={{0,4},{2,6},{4,0},{6,2},{1,5},{3,7},{5,1},{7,3},{8,12},{10,14},{12... | collective-permute-start | bytes 1572872 | tf_op jit(solution)/shard_map/ppermute | solution.py:21
  51.6 20.6 %collective-permute-start.11 = (bf16[2,8,16,1024]{3,2,1,0:T(8,128)(2,1)S(1)}, bf16[2,8,16,1024]{3,2,1,0:T(8,128)(2,1)S(1)}, u32[]{:S(2)}, u32[]{:S(2)}) collective-permute-start(bf16[2,8,16,1024]{3,2,1,0:T(8,128)(2,1)S(1)} %bitcast.108), channel_id=1, source_target_pairs={{0,1},{1,0},{2,3},{3,2},{4,5},{5,4},{6,7},{7,6},{8,9},{9,8},{10,11... | collective-permute-start | bytes 1572872 | tf_op jit(solution)/shard_map/ppermute | solution.py:21
  54.5 19.0 %collective-permute-start.16 = (bf16[192,1024]{1,0:T(8,128)(2,1)S(1)}, bf16[192,1024]{1,0:T(8,128)(2,1)S(1)}, u32[]{:S(2)}, u32[]{:S(2)}) collective-permute-start(bf16[192,1024]{1,0:T(8,128)(2,1)S(1)} %copy-done), channel_id=1, source_target_pairs={{0,24},{8,0},{16,8},{24,16},{1,25},{9,1},{17,9},{25,17},{2,26},{10... | collective-permute-start | bytes 1179656 | tf_op jit(solution)/shard_map/ppermute | solution.py:21
  54.5 19.6 %collective-permute-start.22 = (bf16[192,1024]{1,0:T(8,128)(2,1)S(1)}, bf16[192,1024]{1,0:T(8,128)(2,1)S(1)}, u32[]{:S(2)}, u32[]{:S(2)}) collective-permute-start(bf16[192,1024]{1,0:T(8,128)(2,1)S(1)} %copy-done), channel_id=1, source_target_pairs={{0,1},{1,0},{2,3},{3,2},{4,5},{5,4},{6,7},{7,6},{8,9},{9,8},{10,11... | collective-permute-start | bytes 1179656 | tf_op jit(solution)/shard_map/ppermute | solution.py:21
  60.9 15.9 %collective-permute-start.19 = (bf16[192,1024]{1,0:T(8,128)(2,1)S(1)}, bf16[192,1024]{1,0:T(8,128)(2,1)S(1)}, u32[]{:S(2)}, u32[]{:S(2)}) collective-permute-start(bf16[192,1024]{1,0:T(8,128)(2,1)S(1)} %collective-permute-done.18.refs_12_), channel_id=1, source_target_pairs={{0,24},{8,0},{16,8},{24,16},{1,25},{9,1},{17,9},{25,17},{2,26},{10... | collective-permute-start | bytes 1179656 | tf_op jit(solution)/shard_map/ppermute | solution.py:21
  71.6 12.9 %collective-permute-start.20 = (bf16[192,1024]{1,0:T(8,128)(2,1)S(1)}, bf16[192,1024]{1,0:T(8,128)(2,1)S(1)}, u32[]{:S(2)}, u32[]{:S(2)}) collective-permute-start(bf16[192,1024]{1,0:T(8,128)(2,1)S(1)} %collective-permute-done.15.refs_9_), channel_id=1, source_target_pairs={{0,96},{96,0},{32,64},{64,32},{1,97},{97,1},{33,65},{65,33},{2,98}... | collective-permute-start | bytes 1179656 | tf_op jit(solution)/shard_map/ppermute | solution.py:25
  72.2 12.3 %collective-permute-start.12 = (bf16[2,8,16,1024]{3,2,1,0:T(8,128)(2,1)S(1)}, bf16[2,8,16,1024]{3,2,1,0:T(8,128)(2,1)S(1)}, u32[]{:S(2)}, u32[]{:S(2)}) collective-permute-start(bf16[2,8,16,1024]{3,2,1,0:T(8,128)(2,1)S(1)} %collective-permute-done.8), channel_id=1, source_target_pairs={{0,1},{1,0},{2,3},{3,2},{4,5},{5,4},{6,7},{7,6},{8,9},{9,8},{10,11... | collective-permute-start | bytes 1572872 | tf_op jit(solution)/shard_map/ppermute | solution.py:21
  73.5 16.2 %collective-permute-start.23 = (bf16[192,1024]{1,0:T(8,128)(2,1)S(1)}, bf16[192,1024]{1,0:T(8,128)(2,1)S(1)}, u32[]{:S(2)}, u32[]{:S(2)}) collective-permute-start(bf16[192,1024]{1,0:T(8,128)(2,1)S(1)} %collective-permute-done.15.refs_9_), channel_id=1, source_target_pairs={{0,1},{1,0},{2,3},{3,2},{4,5},{5,4},{6,7},{7,6},{8,9},{9,8},{10,11... | collective-permute-start | bytes 1179656 | tf_op jit(solution)/shard_map/ppermute | solution.py:21
  74.0 15.6 %collective-permute-start.21 = (bf16[192,1024]{1,0:T(8,128)(2,1)S(1)}, bf16[192,1024]{1,0:T(8,128)(2,1)S(1)}, u32[]{:S(2)}, u32[]{:S(2)}) collective-permute-start(bf16[192,1024]{1,0:T(8,128)(2,1)S(1)} %collective-permute-done.17.refs_11_), channel_id=1, source_target_pairs={{0,96},{96,0},{32,64},{64,32},{1,97},{97,1},{33,65},{65,33},{2,98}... | collective-permute-start | bytes 1179656 | tf_op jit(solution)/shard_map/ppermute | solution.py:25
  76.7 13.4 %collective-permute-start.25 = (bf16[192,1024]{1,0:T(8,128)(2,1)S(1)}, bf16[192,1024]{1,0:T(8,128)(2,1)S(1)}, u32[]{:S(2)}, u32[]{:S(2)}) collective-permute-start(bf16[192,1024]{1,0:T(8,128)(2,1)S(1)} %collective-permute-done.17.refs_11_), channel_id=1, source_target_pairs={{0,1},{1,0},{2,3},{3,2},{4,5},{5,4},{6,7},{7,6},{8,9},{9,8},{10,11... | collective-permute-start | bytes 1179656 | tf_op jit(solution)/shard_map/ppermute | solution.py:21
  84.5 5.9 %collective-permute-start.13 = (bf16[2,8,16,1024]{3,2,1,0:T(8,128)(2,1)S(1)}, bf16[2,8,16,1024]{3,2,1,0:T(8,128)(2,1)S(1)}, u32[]{:S(2)}, u32[]{:S(2)}) collective-permute-start(bf16[2,8,16,1024]{3,2,1,0:T(8,128)(2,1)S(1)} %collective-permute-done.9), channel_id=1, source_target_pairs={{0,1},{1,0},{2,3},{3,2},{4,5},{5,4},{6,7},{7,6},{8,9},{9,8},{10,11... | collective-permute-start | bytes 1572872 | tf_op jit(solution)/shard_map/ppermute | solution.py:21
  84.5 6.2 %collective-permute-start.14 = (bf16[2,8,16,1024]{3,2,1,0:T(8,128)(2,1)S(1)}, bf16[2,8,16,1024]{3,2,1,0:T(8,128)(2,1)S(1)}, u32[]{:S(2)}, u32[]{:S(2)}) collective-permute-start(bf16[2,8,16,1024]{3,2,1,0:T(8,128)(2,1)S(1)} %collective-permute-done.10), channel_id=1, source_target_pairs={{0,1},{1,0},{2,3},{3,2},{4,5},{5,4},{6,7},{7,6},{8,9},{9,8},{10,11... | collective-permute-start | bytes 1572872 | tf_op jit(solution)/shard_map/ppermute | solution.py:21
  89.6 2.6 %collective-permute-start.26 = (bf16[192,1024]{1,0:T(8,128)(2,1)S(1)}, bf16[192,1024]{1,0:T(8,128)(2,1)S(1)}, u32[]{:S(2)}, u32[]{:S(2)}) collective-permute-start(bf16[192,1024]{1,0:T(8,128)(2,1)S(1)} %collective-permute-done.18.refs_12_), channel_id=1, source_target_pairs={{0,1},{1,0},{2,3},{3,2},{4,5},{5,4},{6,7},{7,6},{8,9},{9,8},{10,11... | collective-permute-start | bytes 1179656 | tf_op jit(solution)/shard_map/ppermute | solution.py:21
  89.7 2.6 %collective-permute-start.24 = (bf16[192,1024]{1,0:T(8,128)(2,1)S(1)}, bf16[192,1024]{1,0:T(8,128)(2,1)S(1)}, u32[]{:S(2)}, u32[]{:S(2)}) collective-permute-start(bf16[192,1024]{1,0:T(8,128)(2,1)S(1)} %collective-permute-done.16.refs_10_), channel_id=1, source_target_pairs={{0,1},{1,0},{2,3},{3,2},{4,5},{5,4},{6,7},{7,6},{8,9},{9,8},{10,11... | collective-permute-start | bytes 1179656 | tf_op jit(solution)/shard_map/ppermute | solution.py:21
  90.2 2.3 %collective-permute-start.27 = (bf16[192,1024]{1,0:T(8,128)(2,1)S(1)}, bf16[192,1024]{1,0:T(8,128)(2,1)S(1)}, u32[]{:S(2)}, u32[]{:S(2)}) collective-permute-start(bf16[192,1024]{1,0:T(8,128)(2,1)S(1)} %collective-permute-done.19.refs_13_), channel_id=1, source_target_pairs={{0,1},{1,0},{2,3},{3,2},{4,5},{5,4},{6,7},{7,6},{8,9},{9,8},{10,11... | collective-permute-start | bytes 1179656 | tf_op jit(solution)/shard_map/ppermute | solution.py:21
  90.4 2.6 %collective-permute-start.28 = (bf16[192,1024]{1,0:T(8,128)(2,1)S(1)}, bf16[192,1024]{1,0:T(8,128)(2,1)S(1)}, u32[]{:S(2)}, u32[]{:S(2)}) collective-permute-start(bf16[192,1024]{1,0:T(8,128)(2,1)S(1)} %collective-permute-done.20.refs_14_), channel_id=1, source_target_pairs={{0,1},{1,0},{2,3},{3,2},{4,5},{5,4},{6,7},{7,6},{8,9},{9,8},{10,11... | collective-permute-start | bytes 1179656 | tf_op jit(solution)/shard_map/ppermute | solution.py:21
  90.7 2.9 %collective-permute-start.29 = (bf16[192,1024]{1,0:T(8,128)(2,1)S(1)}, bf16[192,1024]{1,0:T(8,128)(2,1)S(1)}, u32[]{:S(2)}, u32[]{:S(2)}) collective-permute-start(bf16[192,1024]{1,0:T(8,128)(2,1)S(1)} %collective-permute-done.21.refs_15_), channel_id=1, source_target_pairs={{0,1},{1,0},{2,3},{3,2},{4,5},{5,4},{6,7},{7,6},{8,9},{9,8},{10,11... | collective-permute-start | bytes 1179656 | tf_op jit(solution)/shard_map/ppermute | solution.py:21
  113.7 13.6 %collective-permute-start.30 = (bf16[8,32,768]{2,1,0:T(8,128)(2,1)S(1)}, bf16[8,32,768]{2,1,0:T(8,128)(2,1)S(1)}, u32[]{:S(2)}, u32[]{:S(2)}) collective-permute-start(bf16[8,32,768]{2,1,0:T(8,128)(2,1)S(1)} %get-tuple-element.10), channel_id=1, source_target_pairs={{0,4},{2,6},{4,0},{6,2},{1,5},{3,7},{5,1},{7,3},{8,12},{10,14},{12... | collective-permute-start | bytes 1179656 | tf_op jit(solution)/shard_map/ppermute | solution.py:21
  113.8 21.0 %collective-permute-start.31 = (bf16[8,32,768]{2,1,0:T(8,128)(2,1)S(1)}, bf16[8,32,768]{2,1,0:T(8,128)(2,1)}, u32[]{:S(2)}, u32[]{:S(2)}) collective-permute-start(bf16[8,32,768]{2,1,0:T(8,128)(2,1)S(1)} %get-tuple-element.11), channel_id=1, source_target_pairs={{0,2},{2,4},{4,6},{6,0},{1,3},{3,5},{5,7},{7,1},{8,10},{10,12},{12... | collective-permute-start | bytes 1179656 | tf_op jit(solution)/shard_map/ppermute | solution.py:21
  113.9 20.9 %collective-permute-start.32 = (bf16[8,32,768]{2,1,0:T(8,128)(2,1)S(1)}, bf16[8,32,768]{2,1,0:T(8,128)(2,1)}, u32[]{:S(2)}, u32[]{:S(2)}) collective-permute-start(bf16[8,32,768]{2,1,0:T(8,128)(2,1)S(1)} %get-tuple-element.12), channel_id=1, source_target_pairs={{0,6},{2,0},{4,2},{6,4},{1,7},{3,1},{5,3},{7,5},{8,14},{10,8},{12,... | collective-permute-start | bytes 1179656 | tf_op jit(solution)/shard_map/ppermute | solution.py:21
  136.7 5.5 %copy-start.1 = (f32[2,2]{1,0:T(2,128)S(1)}, f32[2,2]{1,0:T(2,128)}, u32[]{:S(2)}) copy-start(f32[2,2]{1,0:T(2,128)} %param.7) | copy-start | bytes 52
  136.8 2.0 %collective-permute-start.33 = (f32[8,16,1024]{2,1,0:T(8,128)S(1)}, f32[8,16,1024]{2,1,0:T(8,128)S(1)}, u32[]{:S(2)}, u32[]{:S(2)}) collective-permute-start(f32[8,16,1024]{2,1,0:T(8,128)S(1)} %dynamic-slice_bitcast_fusion), channel_id=1, source_target_pairs={{0,1},{1,0},{2,3},{3,2},{4,5},{5,4},{6,7},{7,6},{8,9},{9,8},{10,11... | collective-permute-start | bytes 1572872 | tf_op jit(solution)/shard_map/ppermute | solution.py:21
  138.9 6.8 %collective-permute-start.34 = (f32[2,16,1024]{2,1,0:T(8,128)S(1)}, f32[2,16,1024]{2,1,0:T(8,128)S(1)}, u32[]{:S(2)}, u32[]{:S(2)}) collective-permute-start(f32[2,16,1024]{2,1,0:T(8,128)S(1)} %get-tuple-element.13), channel_id=1, source_target_pairs={{0,8},{8,16},{16,24},{24,0},{1,9},{9,17},{17,25},{25,1},{2,10},{10... | collective-permute-start | bytes 393224 | tf_op jit(solution)/shard_map/ppermute | solution.py:21
  138.9 8.8 %collective-permute-start.35 = (f32[2,16,1024]{2,1,0:T(8,128)S(1)}, f32[2,16,1024]{2,1,0:T(8,128)S(1)}, u32[]{:S(2)}, u32[]{:S(2)}) collective-permute-start(f32[2,16,1024]{2,1,0:T(8,128)S(1)} %get-tuple-element.15), channel_id=1, source_target_pairs={{0,24},{8,0},{16,8},{24,16},{1,25},{9,1},{17,9},{25,17},{2,26},{10... | collective-permute-start | bytes 393224 | tf_op jit(solution)/shard_map/ppermute | solution.py:21
  142.2 6.5 %collective-permute-start.36 = (f32[2,16,1024]{2,1,0:T(8,128)S(1)}, f32[2,16,1024]{2,1,0:T(8,128)S(1)}, u32[]{:S(2)}, u32[]{:S(2)}) collective-permute-start(f32[2,16,1024]{2,1,0:T(8,128)S(1)} %get-tuple-element.14), channel_id=1, source_target_pairs={{0,16},{8,24},{16,0},{24,8},{1,17},{9,25},{17,1},{25,9},{2,18},{10... | collective-permute-start | bytes 393224 | tf_op jit(solution)/shard_map/ppermute | solution.py:21
  148.7 4.8 %collective-permute-start.37 = (f32[16,1024]{1,0:T(8,128)S(1)}, f32[16,1024]{1,0:T(8,128)S(1)}, u32[]{:S(2)}, u32[]{:S(2)}) collective-permute-start(f32[16,1024]{1,0:T(8,128)S(1)} %get-tuple-element.16), channel_id=1, source_target_pairs={{0,64},{64,0},{1,65},{65,1},{2,66},{66,2},{3,67},{67,3},{4,68},{68... | collective-permute-start | bytes 196616 | tf_op jit(solution)/shard_map/ppermute | solution.py:21
  148.8 5.8 %collective-permute-start.38 = (f32[16,1024]{1,0:T(8,128)S(1)}, f32[16,1024]{1,0:T(8,128)S(1)}, u32[]{:S(2)}, u32[]{:S(2)}) collective-permute-start(f32[16,1024]{1,0:T(8,128)S(1)} %get-tuple-element.18), channel_id=1, source_target_pairs={{0,32},{32,0},{1,33},{33,1},{2,34},{34,2},{3,35},{35,3},{4,36},{36... | collective-permute-start | bytes 196616 | tf_op jit(solution)/shard_map/ppermute | solution.py:21
  150.6 5.5 %collective-permute-start.39 = (f32[16,1024]{1,0:T(8,128)S(1)}, f32[16,1024]{1,0:T(8,128)S(1)}, u32[]{:S(2)}, u32[]{:S(2)}) collective-permute-start(f32[16,1024]{1,0:T(8,128)S(1)} %get-tuple-element.17), channel_id=1, source_target_pairs={{0,96},{96,0},{32,64},{64,32},{1,97},{97,1},{33,65},{65,33},{2,98}... | collective-permute-start | bytes 196616 | tf_op jit(solution)/shard_map/ppermute | solution.py:25
where the time goes:
time: 157 us
  waiting for transfers between devices  78.7 us (50%)
  starting transfers between devices  45.3 us (29%)
  Pallas kernels  21.2 us (14%)
  matrix products  5.54 us (4%)
  local copies, waits for them, and re-layouts  2.35 us (1%)
  other arithmetic  2.13 us (1%)
    ppermute x36, waiting for transfers between devices, shift(): return lax.ppermute(v, axis, [(i, (i + step) % n) for i in range(n)])  66.2 us
    ppermute x36, starting transfers between devices, shift(): return lax.ppermute(v, axis, [(i, (i + step) % n) for i in range(n)])  35.7 us
    pallas_call x1, Pallas kernels, main(): pl.pallas_call(kernel, out_shape=[jax.ShapeDtypeStruct((8, 32, s_rows), B...  20.1 us
    ppermute x4, waiting for transfers between devices, far_z(): return lax.ppermute(v, ('tm', 'zh'), [(0, 3), (3, 0), (1, 2), (2, 1)])  12.5 us
    ppermute x4, starting transfers between devices, far_z(): return lax.ppermute(v, ('tm', 'zh'), [(0, 3), (3, 0), (1, 2), (2, 1)])  9.59 us
    dot_general x8, matrix products, nt(): lax.dot_general(a, b, (((1,), (1,)), ((), ())), preferred_element_type=F32)  4.97 us
  transfers between devices with their start and end apart: 40, of which 24 were waited for; matrix products, arithmetic and copies ran while one was open for 4% of the time, Pallas kernels for 1%

commit v1 on v0

--- a/solution.py
+++ b/solution.py
@@ -147,8 +147,10 @@
     )(*chunks, *pieces)
 
 
-def gather_x(v):
-    return [v, shift(v, "x", 1), shift(v, "x", -1), shift(v, "x", 2)]
+def gather_green_x(v):
+    xm, xp = shift(v, "x", 1), shift(v, "x", -1)
+    far = jnp.stack([shift(xm[0], "x", 1), shift(xp[1], "x", -1)])
+    return [v, xm, xp, far]
 
 
 def both_cores(parts):
@@ -166,12 +168,11 @@
 
 
 def gather_points_yz(b):
-    zb = far_z(b)
-    ym, yp, far = shift(b, "y", 1), shift(b, "y", -1), shift(b, "y", 2)
-    zm = far_z(ym)
+    far = shift(b, "y", 2)
+    pair = jnp.concatenate([b, far_z(b)])
+    ym, yp = shift(pair, "y", 1), shift(pair, "y", -1)
     zfar = far_z(far)
-    zp = shift(zb, "y", -1)
-    return [b, ym, yp, far, zb, zp, zm, zfar]
+    return [pair, far, ym, zfar, yp]
 
 
 def gather_green_yz(g):
@@ -228,12 +229,17 @@
 
 
 def shards(occupied_green, empty_green, basis, time_weights):
-    green = jnp.stack([occupied_green[0], empty_green[0]])
+    lowest = jnp.array(-jnp.inf, BF)
+    none, both = (0, 0, 0), (0, 1, 0)
+    green = jnp.maximum(
+        lax.pad(occupied_green, lowest, (both, none, none)),
+        lax.pad(empty_green, lowest, ((1, 0, 0), none, none)),
+    )
     green = gather_green_yz(green)
     s_pieces = gather_points_x(basis)
     s_block = assemble(s_pieces)
     r_pieces = both_cores(gather_points_yz(basis))
-    greens = both_cores(gather_x(green))
+    greens = both_cores(gather_green_x(green))
     chunks = [project(v, s_block) for v in greens]
     parts = main(chunks, r_pieces, s_block.shape[0])
     coef = jnp.dot(sum_over_x(parts), s_block, preferred_element_type=F32)

time: 157 us -> 130 us (0.83)
  waiting for transfers between devices: 78.7 us -> 51.6 us
  Pallas kernels: 21.2 us -> 19 us
  other arithmetic: 2.13 us -> 3.78 us
    ppermute x36 -> x33, waiting for transfers between devices: 66.2 us -> 49.1 us  [shift(): return lax.ppermute(v, axis, [(i, (i + step) % n) for i in range(n)])]
    ppermute x4 -> x3, waiting for transfers between devices: 12.5 us -> 2.5 us  [far_z(): return lax.ppermute(v, ('tm', 'zh'), [(0, 3), (3, 0), (1, 2), (2, 1)])]
    ppermute x36 -> x33, starting transfers between devices: 35.7 us -> 42.6 us  [shift(): return lax.ppermute(v, axis, [(i, (i + step) % n) for i in range(n)])]
    ppermute x4 -> x3, starting transfers between devices: 9.59 us -> 3.95 us  [far_z(): return lax.ppermute(v, ('tm', 'zh'), [(0, 3), (3, 0), (1, 2), (2, 1)])]
    pallas_call x1, Pallas kernels: 20.1 us -> 17.9 us  [main(): pl.pallas_call(kernel, out_shape=[jax.ShapeDtypeStruct((8, 32, s_rows), B...]
  transfers between devices with their start and end apart: 40 -> 36, of which waited for: 24 -> 17; matrix products, arithmetic and copies ran while one was open for 4% -> 6% of each run, Pallas kernels for 1% -> 1%
where the time goes in v1:
time: 130 us
  waiting for transfers between devices  51.6 us (40%)
  starting transfers between devices  46.6 us (36%)
  Pallas kernels  19 us (15%)
  matrix products  5.51 us (4%)
  other arithmetic  3.78 us (3%)
  local copies, waits for them, and re-layouts  1.81 us (1%)
  between operations  1.55 us (1%)
    ppermute x33, waiting for transfers between devices, shift(): return lax.ppermute(v, axis, [(i, (i + step) % n) for i in range(n)])  49.1 us
    ppermute x33, starting transfers between devices, shift(): return lax.ppermute(v, axis, [(i, (i + step) % n) for i in range(n)])  42.6 us
    pallas_call x1, Pallas kernels, main(): pl.pallas_call(kernel, out_shape=[jax.ShapeDtypeStruct((8, 32, s_rows), B...  17.9 us
    dot_general x8, matrix products, nt(): lax.dot_general(a, b, (((1,), (1,)), ((), ())), preferred_element_type=F32)  4.94 us
    ppermute x3, starting transfers between devices, far_z(): return lax.ppermute(v, ('tm', 'zh'), [(0, 3), (3, 0), (1, 2), (2, 1)])  3.95 us
  transfers between devices with their start and end apart: 36, of which 17 were waited for; matrix products, arithmetic and copies ran while one was open for 6% of the time, Pallas kernels for 1%

profile of v1, /device:TPU:0, one launch (start us, length us, event | category | flops | bytes accessed | tf_op | source)
XLA Modules:
  0.0 129.9 jit_solution(10369492167721076946)
XLA Ops:
  0.0 0.8 pad_maximum_fusion.2
  0.8 4.1 %collective-permute-start = (bf16[2,16,1024]{2,1,0:T(8,128)(2,1)S(1)}, bf16[2,16,1024]{2,1,0:T(8,128)(2,1)S(1)}, u32[]{:S(2)}, u32[]{:S(2)}) collective-permute-start(bf16[2,16,1024]{2,1,0:T(8,128)(2,1)S(1)} %pad_maximum_fusion.2), channel_id=1, source_target_pairs={{0,32},{32,0},{1,33},{33,1},{2,34},{34,2},{3,35},{35,3},{4,36},{36... | collective-permute-start | bytes 196616 | tf_op jit(solution)/shard_map/ppermute | solution.py:21
  4.9 1.5 %collective-permute-start.4 = (bf16[192,1024]{1,0:T(8,128)(2,1)}, bf16[192,1024]{1,0:T(8,128)(2,1)S(1)}, u32[]{:S(2)}, u32[]{:S(2)}) collective-permute-start(bf16[192,1024]{1,0:T(8,128)(2,1)} %refs_0_.1), channel_id=1, source_target_pairs={{0,2},{2,4},{4,6},{6,0},{1,3},{3,5},{5,7},{7,1},{8,10},{10,12},{12... | collective-permute-start | bytes 1179656 | tf_op jit(solution)/shard_map/ppermute | solution.py:21
  6.4 1.7 %collective-permute-start.5 = (bf16[192,1024]{1,0:T(8,128)(2,1)}, bf16[192,1024]{1,0:T(8,128)(2,1)S(1)}, u32[]{:S(2)}, u32[]{:S(2)}) collective-permute-start(bf16[192,1024]{1,0:T(8,128)(2,1)} %refs_0_.1), channel_id=1, source_target_pairs={{0,6},{2,0},{4,2},{6,4},{1,7},{3,1},{5,3},{7,5},{8,14},{10,8},{12,... | collective-permute-start | bytes 1179656 | tf_op jit(solution)/shard_map/ppermute | solution.py:21
  8.1 0.7 collective-permute-start.16
  8.8 0.8 select_bitcast_fusion.1
  9.7 3.1 %collective-permute-start.1 = (bf16[2,2,16,1024]{3,2,1,0:T(8,128)(2,1)S(1)}, bf16[2,2,16,1024]{3,2,1,0:T(8,128)(2,1)S(1)}, u32[]{:S(2)}, u32[]{:S(2)}) collective-permute-start(bf16[2,2,16,1024]{3,2,1,0:T(8,128)(2,1)S(1)} %pad_maximum_fusion.1), channel_id=1, source_target_pairs={{0,24},{8,0},{16,8},{24,16},{1,25},{9,1},{17,9},{25,17},{2,26},{10... | collective-permute-start | bytes 393224 | tf_op jit(solution)/shard_map/ppermute | solution.py:21
  12.7 0.9 constant_dynamic-slice_fusion
  13.7 1.9 %collective-permute-start.6 = (bf16[96,1024]{1,0:T(8,128)(2,1)S(1)}, bf16[96,1024]{1,0:T(8,128)(2,1)S(1)}, u32[]{:S(2)}, u32[]{:S(2)}) collective-permute-start(bf16[96,1024]{1,0:T(8,128)(2,1)S(1)} %constant_dynamic-slice_fusion), channel_id=1, source_target_pairs={{0,4},{2,6},{4,0},{6,2},{1,5},{3,7},{5,1},{7,3},{8,12},{10,14},{12... | collective-permute-start | bytes 589832 | tf_op jit(solution)/shard_map/ppermute | solution.py:21
  15.7 2.2 %collective-permute-start.2 = (bf16[2,2,16,1024]{3,2,1,0:T(8,128)(2,1)S(1)}, bf16[2,2,16,1024]{3,2,1,0:T(8,128)(2,1)S(1)}, u32[]{:S(2)}, u32[]{:S(2)}) collective-permute-start(bf16[2,2,16,1024]{3,2,1,0:T(8,128)(2,1)S(1)} %pad_maximum_fusion.1), channel_id=1, source_target_pairs={{0,16},{8,24},{16,0},{24,8},{1,17},{9,25},{17,1},{25,9},{2,18},{10... | collective-permute-start | bytes 393224 | tf_op jit(solution)/shard_map/ppermute | solution.py:21
  17.9 4.3 %collective-permute-done.2 = bf16[2,2,16,1024]{3,2,1,0:T(8,128)(2,1)S(1)} collective-permute-done((bf16[2,2,16,1024]{3,2,1,0:T(8,128)(2,1)S(1)}, bf16[2,2,16,1024]{3,2,1,0:T(8,128)(2,1)S(1)}, u32[]{:S(2)}, u32[]{:S(2)}) %collective-permute-start.2) | collective-permute-done | bytes 131104 | tf_op jit(solution)/shard_map/ppermute | solution.py:21
  22.2 0.5 collective-permute-start.3
  22.8 5.6 %collective-permute-done.3 = bf16[2,2,16,1024]{3,2,1,0:T(8,128)(2,1)S(1)} collective-permute-done((bf16[2,2,16,1024]{3,2,1,0:T(8,128)(2,1)S(1)}, bf16[2,2,16,1024]{3,2,1,0:T(8,128)(2,1)S(1)}, u32[]{:S(2)}, u32[]{:S(2)}) %collective-permute-start.3) | collective-permute-done | bytes 131104 | tf_op jit(solution)/shard_map/ppermute | solution.py:21
  28.4 0.7 collective-permute-start.8
  29.1 1.1 collective-permute-start.7
  30.2 1.2 collective-permute-start.17
  31.4 3.4 %collective-permute-done.7.refs_4_ = bf16[96,1024]{1,0:T(8,128)(2,1)S(1)} collective-permute-done((bf16[96,1024]{1,0:T(8,128)(2,1)S(1)}, bf16[96,1024]{1,0:T(8,128)(2,1)S(1)}, u32[]{:S(2)}, u32[]{:S(2)}) %collective-permute-start.7) | collective-permute-done | bytes 196640 | tf_op jit(solution)/shard_map/ppermute | solution.py:21
  34.8 2.6 %collective-permute-start.9 = (bf16[2,8,16,1024]{3,2,1,0:T(8,128)(2,1)S(1)}, bf16[2,8,16,1024]{3,2,1,0:T(8,128)(2,1)S(1)}, u32[]{:S(2)}, u32[]{:S(2)}) collective-permute-start(bf16[2,8,16,1024]{3,2,1,0:T(8,128)(2,1)S(1)} %bitcast.112), channel_id=1, source_target_pairs={{0,6},{2,0},{4,2},{6,4},{1,7},{3,1},{5,3},{7,5},{8,14},{10,8},{12,... | collective-permute-start | bytes 1572872 | tf_op jit(solution)/shard_map/ppermute | solution.py:21
  37.4 0.1 collective-permute-start.18
  37.5 1.1 assemble.1
  38.6 0.6 convolution_convert_fusion.7
  39.3 0.3 collective-permute-done.17.refs_9_
  39.6 3.0 %collective-permute-start.20 = (bf16[384,1024]{1,0:T(8,128)(2,1)S(1)}, bf16[384,1024]{1,0:T(8,128)(2,1)S(1)}, u32[]{:S(2)}, u32[]{:S(2)}) collective-permute-start(bf16[384,1024]{1,0:T(8,128)(2,1)S(1)} %constant_dynamic-update-slice_fusion.refs_8_), channel_id=1, source_target_pairs={{0,24},{8,0},{16,8},{24,16},{1,25},{9,1},{17,9},{25,17},{2,26},{10... | collective-permute-start | bytes 2359304 | tf_op jit(solution)/shard_map/ppermute | solution.py:21
  42.5 3.2 %collective-permute-start.19 = (bf16[192,1024]{1,0:T(8,128)(2,1)S(1)}, bf16[192,1024]{1,0:T(8,128)(2,1)S(1)}, u32[]{:S(2)}, u32[]{:S(2)}) collective-permute-start(bf16[192,1024]{1,0:T(8,128)(2,1)S(1)} %collective-permute-done.17.refs_9_), channel_id=1, source_target_pairs={{0,96},{96,0},{32,64},{64,32},{1,97},{97,1},{33,65},{65,33},{2,98}... | collective-permute-start | bytes 1179656 | tf_op jit(solution)/shard_map/ppermute | solution.py:25
  45.9 0.6 convolution_convert_fusion.5
  46.5 3.3 %collective-permute-start.11 = (bf16[8,16,1024]{2,1,0:T(8,128)(2,1)S(1)}, bf16[8,16,1024]{2,1,0:T(8,128)(2,1)S(1)}, u32[]{:S(2)}, u32[]{:S(2)}) collective-permute-start(bf16[8,16,1024]{2,1,0:T(8,128)(2,1)S(1)} %slice_bitcast_fusion), channel_id=1, source_target_pairs={{0,6},{2,0},{4,2},{6,4},{1,7},{3,1},{5,3},{7,5},{8,14},{10,8},{12,... | collective-permute-start | bytes 786440 | tf_op jit(solution)/shard_map/ppermute | solution.py:21
  49.8 0.6 convolution_convert_fusion.3
  50.4 4.4 %collective-permute-done.10 = bf16[8,16,1024]{2,1,0:T(8,128)(2,1)S(1)} collective-permute-done((bf16[8,16,1024]{2,1,0:T(8,128)(2,1)S(1)}, bf16[8,16,1024]{2,1,0:T(8,128)(2,1)S(1)}, u32[]{:S(2)}, u32[]{:S(2)}) %collective-permute-start.10) | collective-permute-done | bytes 262176 | tf_op jit(solution)/shard_map/ppermute | solution.py:21
  54.9 0.6 convolution_convert_fusion.6
  55.5 0.6 collective-permute-start.14
  56.1 0.1 collective-permute-start.15
  56.2 0.6 convolution_convert_fusion.4
  56.9 1.7 %collective-permute-done.18.refs_10_ = bf16[384,1024]{1,0:T(8,128)(2,1)S(1)} collective-permute-done((bf16[384,1024]{1,0:T(8,128)(2,1)S(1)}, bf16[384,1024]{1,0:T(8,128)(2,1)S(1)}, u32[]{:S(2)}, u32[]{:S(2)}) %collective-permute-start.18) | collective-permute-done | bytes 786464 | tf_op jit(solution)/shard_map/ppermute | solution.py:21
  58.6 1.1 collective-permute-done.20.refs_12_
  59.7 0.5 collective-permute-start.25
  60.2 0.6 convolution_convert_fusion.2
  60.8 0.1 collective-permute-start.22
  60.9 0.5 collective-permute-start.24
  61.4 0.6 convolution_convert_fusion.1
  62.0 0.6 convolution_convert_fusion
  62.7 1.0 collective-permute-done.22.refs_14_
  63.7 0.6 collective-permute-done.24.refs_16_
  64.2 17.9 %main.1 = (bf16[8,32,768]{2,1,0:T(8,128)(2,1)S(1)}, bf16[8,32,768]{2,1,0:T(8,128)(2,1)S(1)}, bf16[8,32,768]{2,1,0:T(8,128)(2,1)S(1)}, bf16[8,32,768]{2,1,0:T(8,128)(2,1)S(1)}) custom-call(bf16[2,8,16,768]{3,2,1,0:T(8,128)(2,1)S(1)} %bitcast.101, bf16[2,8,16,768]{3,2,1,0:T(8,128)(2,1)S(1)} %bitcast.104, bf16[2,8,16,768]{3,2,1,0:T(8,128)(2,1)S(1)} %bitcast.102, ...), custom_call_target="tpu_custom_call" | custom-call | flops 14495514624 | bytes 12582912 | tf_op jit(solution)/shard_map/main/pallas_call | solution.py:129
  82.2 0.6 collective-permute-start.26
  82.8 1.8 %collective-permute-start.27 = (bf16[8,32,768]{2,1,0:T(8,128)(2,1)S(1)}, bf16[8,32,768]{2,1,0:T(8,128)(2,1)}, u32[]{:S(2)}, u32[]{:S(2)}) collective-permute-start(bf16[8,32,768]{2,1,0:T(8,128)(2,1)S(1)} %get-tuple-element.11), channel_id=1, source_target_pairs={{0,2},{2,4},{4,6},{6,0},{1,3},{3,5},{5,7},{7,1},{8,10},{10,12},{12... | collective-permute-start | bytes 1179656 | tf_op jit(solution)/shard_map/ppermute | solution.py:21
  84.6 1.4 %collective-permute-start.28 = (bf16[8,32,768]{2,1,0:T(8,128)(2,1)S(1)}, bf16[8,32,768]{2,1,0:T(8,128)(2,1)}, u32[]{:S(2)}, u32[]{:S(2)}) collective-permute-start(bf16[8,32,768]{2,1,0:T(8,128)(2,1)S(1)} %get-tuple-element.12), channel_id=1, source_target_pairs={{0,6},{2,0},{4,2},{6,4},{1,7},{3,1},{5,3},{7,5},{8,14},{10,8},{12,... | collective-permute-start | bytes 1179656 | tf_op jit(solution)/shard_map/ppermute | solution.py:21
  86.0 9.8 %collective-permute-done.26 = bf16[8,32,768]{2,1,0:T(8,128)(2,1)S(1)} collective-permute-done((bf16[8,32,768]{2,1,0:T(8,128)(2,1)S(1)}, bf16[8,32,768]{2,1,0:T(8,128)(2,1)S(1)}, u32[]{:S(2)}, u32[]{:S(2)}) %collective-permute-start.26) | collective-permute-done | bytes 393248 | tf_op jit(solution)/shard_map/ppermute | solution.py:21
  95.8 7.6 %collective-permute-done.27 = bf16[8,32,768]{2,1,0:T(8,128)(2,1)} collective-permute-done((bf16[8,32,768]{2,1,0:T(8,128)(2,1)S(1)}, bf16[8,32,768]{2,1,0:T(8,128)(2,1)}, u32[]{:S(2)}, u32[]{:S(2)}) %collective-permute-start.27) | collective-permute-done | bytes 393248 | tf_op jit(solution)/shard_map/ppermute | solution.py:21
  103.4 1.3 %add_convert_fusion = bf16[8,32,768]{2,1,0:T(8,128)(2,1)S(1)} fusion(bf16[8,32,768]{2,1,0:T(8,128)(2,1)} %collective-permute-done.28, bf16[8,32,768]{2,1,0:T(8,128)(2,1)} %collective-permute-done.27, bf16[8,32,768]{2,1,0:T(8,128)(2,1)S(1)} %collective-permute-done.26, bf16[8,32,768]{2,1,0:T(8,128)(2,1)S(1)} %get-tuple-element.9), kind=kLoop, calls=%fused_computation.10 | loop fusion | flops 1572864 | bytes 1966080 | tf_op jit(solution)/shard_map/convert_element_type | solution.py:199
  104.7 0.6 fusion
  105.4 0.1 collective-permute-start.29
  105.5 1.9 %collective-permute-done.29 = f32[8,16,1024]{2,1,0:T(8,128)S(1)} collective-permute-done((f32[8,16,1024]{2,1,0:T(8,128)S(1)}, f32[8,16,1024]{2,1,0:T(8,128)S(1)}, u32[]{:S(2)}, u32[]{:S(2)}) %collective-permute-start.29) | collective-permute-done | bytes 524320 | tf_op jit(solution)/shard_map/ppermute | solution.py:21
  107.5 1.0 collective-permute-start.30
  108.5 2.8 %collective-permute-start.31 = (f32[2,16,1024]{2,1,0:T(8,128)S(1)}, f32[2,16,1024]{2,1,0:T(8,128)S(1)}, u32[]{:S(2)}, u32[]{:S(2)}) collective-permute-start(f32[2,16,1024]{2,1,0:T(8,128)S(1)} %get-tuple-element.15), channel_id=1, source_target_pairs={{0,24},{8,0},{16,8},{24,16},{1,25},{9,1},{17,9},{25,17},{2,26},{10... | collective-permute-start | bytes 393224 | tf_op jit(solution)/shard_map/ppermute | solution.py:21
  111.3 1.4 %collective-permute-start.32 = (f32[2,16,1024]{2,1,0:T(8,128)S(1)}, f32[2,16,1024]{2,1,0:T(8,128)S(1)}, u32[]{:S(2)}, u32[]{:S(2)}) collective-permute-start(f32[2,16,1024]{2,1,0:T(8,128)S(1)} %get-tuple-element.14), channel_id=1, source_target_pairs={{0,16},{8,24},{16,0},{24,8},{1,17},{9,25},{17,1},{25,9},{2,18},{10... | collective-permute-start | bytes 393224 | tf_op jit(solution)/shard_map/ppermute | solution.py:21
  112.7 0.6 fusion.7
  114.5 0.5 collective-permute-done.30
  115.0 2.2 %collective-permute-done.31 = f32[2,16,1024]{2,1,0:T(8,128)S(1)} collective-permute-done((f32[2,16,1024]{2,1,0:T(8,128)S(1)}, f32[2,16,1024]{2,1,0:T(8,128)S(1)}, u32[]{:S(2)}, u32[]{:S(2)}) %collective-permute-start.31) | collective-permute-done | bytes 131104 | tf_op jit(solution)/shard_map/ppermute | solution.py:21
  117.2 1.8 %collective-permute-done.32 = f32[2,16,1024]{2,1,0:T(8,128)S(1)} collective-permute-done((f32[2,16,1024]{2,1,0:T(8,128)S(1)}, f32[2,16,1024]{2,1,0:T(8,128)S(1)}, u32[]{:S(2)}, u32[]{:S(2)}) %collective-permute-start.32) | collective-permute-done | bytes 131104 | tf_op jit(solution)/shard_map/ppermute | solution.py:21
  119.0 1.1 collective-permute-start.33
  120.2 3.6 %collective-permute-start.34 = (f32[16,1024]{1,0:T(8,128)S(1)}, f32[16,1024]{1,0:T(8,128)S(1)}, u32[]{:S(2)}, u32[]{:S(2)}) collective-permute-start(f32[16,1024]{1,0:T(8,128)S(1)} %get-tuple-element.18), channel_id=1, source_target_pairs={{0,32},{32,0},{1,33},{33,1},{2,34},{34,2},{3,35},{35,3},{4,36},{36... | collective-permute-start | bytes 196616 | tf_op jit(solution)/shard_map/ppermute | solution.py:21
  123.8 2.9 %collective-permute-done.34 = f32[16,1024]{1,0:T(8,128)S(1)} collective-permute-done((f32[16,1024]{1,0:T(8,128)S(1)}, f32[16,1024]{1,0:T(8,128)S(1)}, u32[]{:S(2)}, u32[]{:S(2)}) %collective-permute-start.34) | collective-permute-done | bytes 65568 | tf_op jit(solution)/shard_map/ppermute | solution.py:21
  126.8 2.5 %collective-permute-done.35 = f32[16,1024]{1,0:T(8,128)S(1)} collective-permute-done((f32[16,1024]{1,0:T(8,128)S(1)}, f32[16,1024]{1,0:T(8,128)S(1)}, u32[]{:S(2)}, u32[]{:S(2)}) %collective-permute-start.35) | collective-permute-done | bytes 65568 | tf_op jit(solution)/shard_map/ppermute | solution.py:25
  129.3 0.6 fusion.6
  (45 shorter events, 0.6 us)
Async XLA Ops:
  0.0 30.2 %copy-start = (bf16[192,1024]{1,0:T(8,128)(2,1)S(1)}, bf16[192,1024]{1,0:T(8,128)(2,1)}, u32[]{:S(2)}) copy-start(bf16[192,1024]{1,0:T(8,128)(2,1)} %refs_0_.1) | copy-start | bytes 1179652
  0.8 8.0 %collective-permute-start = (bf16[2,16,1024]{2,1,0:T(8,128)(2,1)S(1)}, bf16[2,16,1024]{2,1,0:T(8,128)(2,1)S(1)}, u32[]{:S(2)}, u32[]{:S(2)}) collective-permute-start(bf16[2,16,1024]{2,1,0:T(8,128)(2,1)S(1)} %pad_maximum_fusion.2), channel_id=1, source_target_pairs={{0,32},{32,0},{1,33},{33,1},{2,34},{34,2},{3,35},{35,3},{4,36},{36... | collective-permute-start | bytes 196616 | tf_op jit(solution)/shard_map/ppermute | solution.py:21
  4.9 32.5 %collective-permute-start.4 = (bf16[192,1024]{1,0:T(8,128)(2,1)}, bf16[192,1024]{1,0:T(8,128)(2,1)S(1)}, u32[]{:S(2)}, u32[]{:S(2)}) collective-permute-start(bf16[192,1024]{1,0:T(8,128)(2,1)} %refs_0_.1), channel_id=1, source_target_pairs={{0,2},{2,4},{4,6},{6,0},{1,3},{3,5},{5,7},{7,1},{8,10},{10,12},{12... | collective-permute-start | bytes 1179656 | tf_op jit(solution)/shard_map/ppermute | solution.py:21
  6.4 31.0 %collective-permute-start.5 = (bf16[192,1024]{1,0:T(8,128)(2,1)}, bf16[192,1024]{1,0:T(8,128)(2,1)S(1)}, u32[]{:S(2)}, u32[]{:S(2)}) collective-permute-start(bf16[192,1024]{1,0:T(8,128)(2,1)} %refs_0_.1), channel_id=1, source_target_pairs={{0,6},{2,0},{4,2},{6,4},{1,7},{3,1},{5,3},{7,5},{8,14},{10,8},{12,... | collective-permute-start | bytes 1179656 | tf_op jit(solution)/shard_map/ppermute | solution.py:21
  8.1 22.1 %collective-permute-start.16 = (bf16[192,1024]{1,0:T(8,128)(2,1)}, bf16[192,1024]{1,0:T(8,128)(2,1)S(1)}, u32[]{:S(2)}, u32[]{:S(2)}) collective-permute-start(bf16[192,1024]{1,0:T(8,128)(2,1)} %refs_0_.1), channel_id=1, source_target_pairs={{0,96},{96,0},{32,64},{64,32},{1,97},{97,1},{33,65},{65,33},{2,98}... | collective-permute-start | bytes 1179656 | tf_op jit(solution)/shard_map/ppermute | solution.py:25
  9.7 6.0 %collective-permute-start.1 = (bf16[2,2,16,1024]{3,2,1,0:T(8,128)(2,1)S(1)}, bf16[2,2,16,1024]{3,2,1,0:T(8,128)(2,1)S(1)}, u32[]{:S(2)}, u32[]{:S(2)}) collective-permute-start(bf16[2,2,16,1024]{3,2,1,0:T(8,128)(2,1)S(1)} %pad_maximum_fusion.1), channel_id=1, source_target_pairs={{0,24},{8,0},{16,8},{24,16},{1,25},{9,1},{17,9},{25,17},{2,26},{10... | collective-permute-start | bytes 393224 | tf_op jit(solution)/shard_map/ppermute | solution.py:21
  13.7 15.4 %collective-permute-start.6 = (bf16[96,1024]{1,0:T(8,128)(2,1)S(1)}, bf16[96,1024]{1,0:T(8,128)(2,1)S(1)}, u32[]{:S(2)}, u32[]{:S(2)}) collective-permute-start(bf16[96,1024]{1,0:T(8,128)(2,1)S(1)} %constant_dynamic-slice_fusion), channel_id=1, source_target_pairs={{0,4},{2,6},{4,0},{6,2},{1,5},{3,7},{5,1},{7,3},{8,12},{10,14},{12... | collective-permute-start | bytes 589832 | tf_op jit(solution)/shard_map/ppermute | solution.py:21
  15.7 6.6 %collective-permute-start.2 = (bf16[2,2,16,1024]{3,2,1,0:T(8,128)(2,1)S(1)}, bf16[2,2,16,1024]{3,2,1,0:T(8,128)(2,1)S(1)}, u32[]{:S(2)}, u32[]{:S(2)}) collective-permute-start(bf16[2,2,16,1024]{3,2,1,0:T(8,128)(2,1)S(1)} %pad_maximum_fusion.1), channel_id=1, source_target_pairs={{0,16},{8,24},{16,0},{24,8},{1,17},{9,25},{17,1},{25,9},{2,18},{10... | collective-permute-start | bytes 393224 | tf_op jit(solution)/shard_map/ppermute | solution.py:21
  22.2 6.2 %collective-permute-start.3 = (bf16[2,2,16,1024]{3,2,1,0:T(8,128)(2,1)S(1)}, bf16[2,2,16,1024]{3,2,1,0:T(8,128)(2,1)S(1)}, u32[]{:S(2)}, u32[]{:S(2)}) collective-permute-start(bf16[2,2,16,1024]{3,2,1,0:T(8,128)(2,1)S(1)} %pad_maximum_fusion.1), channel_id=1, source_target_pairs={{0,8},{8,16},{16,24},{24,0},{1,9},{9,17},{17,25},{25,1},{2,10},{10... | collective-permute-start | bytes 393224 | tf_op jit(solution)/shard_map/ppermute | solution.py:21
  28.4 14.1 %collective-permute-start.8 = (bf16[2,8,16,1024]{3,2,1,0:T(8,128)(2,1)S(1)}, bf16[2,8,16,1024]{3,2,1,0:T(8,128)(2,1)S(1)}, u32[]{:S(2)}, u32[]{:S(2)}) collective-permute-start(bf16[2,8,16,1024]{3,2,1,0:T(8,128)(2,1)S(1)} %bitcast.111), channel_id=1, source_target_pairs={{0,2},{2,4},{4,6},{6,0},{1,3},{3,5},{5,7},{7,1},{8,10},{10,12},{12... | collective-permute-start | bytes 1572872 | tf_op jit(solution)/shard_map/ppermute | solution.py:21
  29.1 5.7 %collective-permute-start.7 = (bf16[96,1024]{1,0:T(8,128)(2,1)S(1)}, bf16[96,1024]{1,0:T(8,128)(2,1)S(1)}, u32[]{:S(2)}, u32[]{:S(2)}) collective-permute-start(bf16[96,1024]{1,0:T(8,128)(2,1)S(1)} %collective-permute-done.6.refs_3_), channel_id=1, source_target_pairs={{0,64},{64,0},{1,65},{65,1},{2,66},{66,2},{3,67},{67,3},{4,68},{68... | collective-permute-start | bytes 589832 | tf_op jit(solution)/shard_map/ppermute | solution.py:21
  30.2 9.4 %collective-permute-start.17 = (bf16[192,1024]{1,0:T(8,128)(2,1)S(1)}, bf16[192,1024]{1,0:T(8,128)(2,1)S(1)}, u32[]{:S(2)}, u32[]{:S(2)}) collective-permute-start(bf16[192,1024]{1,0:T(8,128)(2,1)S(1)} %copy-done), channel_id=1, source_target_pairs={{0,16},{8,24},{16,0},{24,8},{1,17},{9,25},{17,1},{25,9},{2,18},{10... | collective-permute-start | bytes 1179656 | tf_op jit(solution)/shard_map/ppermute | solution.py:21
  34.8 11.0 %collective-permute-start.9 = (bf16[2,8,16,1024]{3,2,1,0:T(8,128)(2,1)S(1)}, bf16[2,8,16,1024]{3,2,1,0:T(8,128)(2,1)S(1)}, u32[]{:S(2)}, u32[]{:S(2)}) collective-permute-start(bf16[2,8,16,1024]{3,2,1,0:T(8,128)(2,1)S(1)} %bitcast.112), channel_id=1, source_target_pairs={{0,6},{2,0},{4,2},{6,4},{1,7},{3,1},{5,3},{7,5},{8,14},{10,8},{12,... | collective-permute-start | bytes 1572872 | tf_op jit(solution)/shard_map/ppermute | solution.py:21
  37.4 9.1 %collective-permute-start.12 = (bf16[2,8,16,1024]{3,2,1,0:T(8,128)(2,1)S(1)}, bf16[2,8,16,1024]{3,2,1,0:T(8,128)(2,1)S(1)}, u32[]{:S(2)}, u32[]{:S(2)}) collective-permute-start(bf16[2,8,16,1024]{3,2,1,0:T(8,128)(2,1)S(1)} %bitcast.113), channel_id=1, source_target_pairs={{0,1},{1,0},{2,3},{3,2},{4,5},{5,4},{6,7},{7,6},{8,9},{9,8},{10,11... | collective-permute-start | bytes 1572872 | tf_op jit(solution)/shard_map/ppermute | solution.py:21
  37.4 21.2 %collective-permute-start.18 = (bf16[384,1024]{1,0:T(8,128)(2,1)S(1)}, bf16[384,1024]{1,0:T(8,128)(2,1)S(1)}, u32[]{:S(2)}, u32[]{:S(2)}) collective-permute-start(bf16[384,1024]{1,0:T(8,128)(2,1)S(1)} %constant_dynamic-update-slice_fusion.refs_8_), channel_id=1, source_target_pairs={{0,8},{8,16},{16,24},{24,0},{1,9},{9,17},{17,25},{25,1},{2,10},{10... | collective-permute-start | bytes 2359304 | tf_op jit(solution)/shard_map/ppermute | solution.py:21
  39.6 20.1 %collective-permute-start.20 = (bf16[384,1024]{1,0:T(8,128)(2,1)S(1)}, bf16[384,1024]{1,0:T(8,128)(2,1)S(1)}, u32[]{:S(2)}, u32[]{:S(2)}) collective-permute-start(bf16[384,1024]{1,0:T(8,128)(2,1)S(1)} %constant_dynamic-update-slice_fusion.refs_8_), channel_id=1, source_target_pairs={{0,24},{8,0},{16,8},{24,16},{1,25},{9,1},{17,9},{25,17},{2,26},{10... | collective-permute-start | bytes 2359304 | tf_op jit(solution)/shard_map/ppermute | solution.py:21
  42.5 13.6 %collective-permute-start.19 = (bf16[192,1024]{1,0:T(8,128)(2,1)S(1)}, bf16[192,1024]{1,0:T(8,128)(2,1)S(1)}, u32[]{:S(2)}, u32[]{:S(2)}) collective-permute-start(bf16[192,1024]{1,0:T(8,128)(2,1)S(1)} %collective-permute-done.17.refs_9_), channel_id=1, source_target_pairs={{0,96},{96,0},{32,64},{64,32},{1,97},{97,1},{33,65},{65,33},{2,98}... | collective-permute-start | bytes 1179656 | tf_op jit(solution)/shard_map/ppermute | solution.py:25
  45.8 9.1 %collective-permute-start.10 = (bf16[8,16,1024]{2,1,0:T(8,128)(2,1)S(1)}, bf16[8,16,1024]{2,1,0:T(8,128)(2,1)S(1)}, u32[]{:S(2)}, u32[]{:S(2)}) collective-permute-start(bf16[8,16,1024]{2,1,0:T(8,128)(2,1)S(1)} %slice_bitcast_fusion.1), channel_id=1, source_target_pairs={{0,2},{2,4},{4,6},{6,0},{1,3},{3,5},{5,7},{7,1},{8,10},{10,12},{12... | collective-permute-start | bytes 786440 | tf_op jit(solution)/shard_map/ppermute | solution.py:21
  46.5 9.0 %collective-permute-start.11 = (bf16[8,16,1024]{2,1,0:T(8,128)(2,1)S(1)}, bf16[8,16,1024]{2,1,0:T(8,128)(2,1)S(1)}, u32[]{:S(2)}, u32[]{:S(2)}) collective-permute-start(bf16[8,16,1024]{2,1,0:T(8,128)(2,1)S(1)} %slice_bitcast_fusion), channel_id=1, source_target_pairs={{0,6},{2,0},{4,2},{6,4},{1,7},{3,1},{5,3},{7,5},{8,14},{10,8},{12,... | collective-permute-start | bytes 786440 | tf_op jit(solution)/shard_map/ppermute | solution.py:21
  54.9 4.8 %collective-permute-start.13 = (bf16[2,8,16,1024]{3,2,1,0:T(8,128)(2,1)S(1)}, bf16[2,8,16,1024]{3,2,1,0:T(8,128)(2,1)S(1)}, u32[]{:S(2)}, u32[]{:S(2)}) collective-permute-start(bf16[2,8,16,1024]{3,2,1,0:T(8,128)(2,1)S(1)} %collective-permute-done.8), channel_id=1, source_target_pairs={{0,1},{1,0},{2,3},{3,2},{4,5},{5,4},{6,7},{7,6},{8,9},{9,8},{10,11... | collective-permute-start | bytes 1572872 | tf_op jit(solution)/shard_map/ppermute | solution.py:21
  55.5 5.3 %collective-permute-start.14 = (bf16[2,8,16,1024]{3,2,1,0:T(8,128)(2,1)S(1)}, bf16[2,8,16,1024]{3,2,1,0:T(8,128)(2,1)S(1)}, u32[]{:S(2)}, u32[]{:S(2)}) collective-permute-start(bf16[2,8,16,1024]{3,2,1,0:T(8,128)(2,1)S(1)} %collective-permute-done.9), channel_id=1, source_target_pairs={{0,1},{1,0},{2,3},{3,2},{4,5},{5,4},{6,7},{7,6},{8,9},{9,8},{10,11... | collective-permute-start | bytes 1572872 | tf_op jit(solution)/shard_map/ppermute | solution.py:21
  56.1 4.8 %collective-permute-start.15 = (bf16[2,8,16,1024]{3,2,1,0:T(8,128)(2,1)S(1)}, bf16[2,8,16,1024]{3,2,1,0:T(8,128)(2,1)S(1)}, u32[]{:S(2)}, u32[]{:S(2)}) collective-permute-start(bf16[2,8,16,1024]{3,2,1,0:T(8,128)(2,1)S(1)} %pad_maximum_fusion), channel_id=1, source_target_pairs={{0,1},{1,0},{2,3},{3,2},{4,5},{5,4},{6,7},{7,6},{8,9},{9,8},{10,11... | collective-permute-start | bytes 1572872 | tf_op jit(solution)/shard_map/ppermute | solution.py:21
  58.6 5.1 %collective-permute-start.21 = (bf16[384,1024]{1,0:T(8,128)(2,1)S(1)}, bf16[384,1024]{1,0:T(8,128)(2,1)S(1)}, u32[]{:S(2)}, u32[]{:S(2)}) collective-permute-start(bf16[384,1024]{1,0:T(8,128)(2,1)S(1)} %constant_dynamic-update-slice_fusion.refs_8_), channel_id=1, source_target_pairs={{0,1},{1,0},{2,3},{3,2},{4,5},{5,4},{6,7},{7,6},{8,9},{9,8},{10,11... | collective-permute-start | bytes 2359304 | tf_op jit(solution)/shard_map/ppermute | solution.py:21
  59.7 4.6 %collective-permute-start.23 = (bf16[384,1024]{1,0:T(8,128)(2,1)S(1)}, bf16[384,1024]{1,0:T(8,128)(2,1)S(1)}, u32[]{:S(2)}, u32[]{:S(2)}) collective-permute-start(bf16[384,1024]{1,0:T(8,128)(2,1)S(1)} %collective-permute-done.18.refs_10_), channel_id=1, source_target_pairs={{0,1},{1,0},{2,3},{3,2},{4,5},{5,4},{6,7},{7,6},{8,9},{9,8},{10,11... | collective-permute-start | bytes 2359304 | tf_op jit(solution)/shard_map/ppermute | solution.py:21
  59.7 4.6 %collective-permute-start.25 = (bf16[384,1024]{1,0:T(8,128)(2,1)S(1)}, bf16[384,1024]{1,0:T(8,128)(2,1)S(1)}, u32[]{:S(2)}, u32[]{:S(2)}) collective-permute-start(bf16[384,1024]{1,0:T(8,128)(2,1)S(1)} %collective-permute-done.20.refs_12_), channel_id=1, source_target_pairs={{0,1},{1,0},{2,3},{3,2},{4,5},{5,4},{6,7},{7,6},{8,9},{9,8},{10,11... | collective-permute-start | bytes 2359304 | tf_op jit(solution)/shard_map/ppermute | solution.py:21
  60.8 2.8 %collective-permute-start.22 = (bf16[192,1024]{1,0:T(8,128)(2,1)S(1)}, bf16[192,1024]{1,0:T(8,128)(2,1)S(1)}, u32[]{:S(2)}, u32[]{:S(2)}) collective-permute-start(bf16[192,1024]{1,0:T(8,128)(2,1)S(1)} %collective-permute-done.17.refs_9_), channel_id=1, source_target_pairs={{0,1},{1,0},{2,3},{3,2},{4,5},{5,4},{6,7},{7,6},{8,9},{9,8},{10,11... | collective-permute-start | bytes 1179656 | tf_op jit(solution)/shard_map/ppermute | solution.py:21
  60.9 3.3 %collective-permute-start.24 = (bf16[192,1024]{1,0:T(8,128)(2,1)S(1)}, bf16[192,1024]{1,0:T(8,128)(2,1)S(1)}, u32[]{:S(2)}, u32[]{:S(2)}) collective-permute-start(bf16[192,1024]{1,0:T(8,128)(2,1)S(1)} %collective-permute-done.19.refs_11_), channel_id=1, source_target_pairs={{0,1},{1,0},{2,3},{3,2},{4,5},{5,4},{6,7},{7,6},{8,9},{9,8},{10,11... | collective-permute-start | bytes 1179656 | tf_op jit(solution)/shard_map/ppermute | solution.py:21
  82.2 13.6 %collective-permute-start.26 = (bf16[8,32,768]{2,1,0:T(8,128)(2,1)S(1)}, bf16[8,32,768]{2,1,0:T(8,128)(2,1)S(1)}, u32[]{:S(2)}, u32[]{:S(2)}) collective-permute-start(bf16[8,32,768]{2,1,0:T(8,128)(2,1)S(1)} %get-tuple-element.10), channel_id=1, source_target_pairs={{0,4},{2,6},{4,0},{6,2},{1,5},{3,7},{5,1},{7,3},{8,12},{10,14},{12... | collective-permute-start | bytes 1179656 | tf_op jit(solution)/shard_map/ppermute | solution.py:21
  82.8 20.6 %collective-permute-start.27 = (bf16[8,32,768]{2,1,0:T(8,128)(2,1)S(1)}, bf16[8,32,768]{2,1,0:T(8,128)(2,1)}, u32[]{:S(2)}, u32[]{:S(2)}) collective-permute-start(bf16[8,32,768]{2,1,0:T(8,128)(2,1)S(1)} %get-tuple-element.11), channel_id=1, source_target_pairs={{0,2},{2,4},{4,6},{6,0},{1,3},{3,5},{5,7},{7,1},{8,10},{10,12},{12... | collective-permute-start | bytes 1179656 | tf_op jit(solution)/shard_map/ppermute | solution.py:21
  84.6 18.8 %collective-permute-start.28 = (bf16[8,32,768]{2,1,0:T(8,128)(2,1)S(1)}, bf16[8,32,768]{2,1,0:T(8,128)(2,1)}, u32[]{:S(2)}, u32[]{:S(2)}) collective-permute-start(bf16[8,32,768]{2,1,0:T(8,128)(2,1)S(1)} %get-tuple-element.12), channel_id=1, source_target_pairs={{0,6},{2,0},{4,2},{6,4},{1,7},{3,1},{5,3},{7,5},{8,14},{10,8},{12,... | collective-permute-start | bytes 1179656 | tf_op jit(solution)/shard_map/ppermute | solution.py:21
  105.3 7.4 %copy-start.1 = (f32[2,2]{1,0:T(2,128)S(1)}, f32[2,2]{1,0:T(2,128)}, u32[]{:S(2)}) copy-start(f32[2,2]{1,0:T(2,128)} %param.7) | copy-start | bytes 52
  105.4 2.0 %collective-permute-start.29 = (f32[8,16,1024]{2,1,0:T(8,128)S(1)}, f32[8,16,1024]{2,1,0:T(8,128)S(1)}, u32[]{:S(2)}, u32[]{:S(2)}) collective-permute-start(f32[8,16,1024]{2,1,0:T(8,128)S(1)} %dynamic-slice_bitcast_fusion), channel_id=1, source_target_pairs={{0,1},{1,0},{2,3},{3,2},{4,5},{5,4},{6,7},{7,6},{8,9},{9,8},{10,11... | collective-permute-start | bytes 1572872 | tf_op jit(solution)/shard_map/ppermute | solution.py:21
  107.5 7.5 %collective-permute-start.30 = (f32[2,16,1024]{2,1,0:T(8,128)S(1)}, f32[2,16,1024]{2,1,0:T(8,128)S(1)}, u32[]{:S(2)}, u32[]{:S(2)}) collective-permute-start(f32[2,16,1024]{2,1,0:T(8,128)S(1)} %get-tuple-element.13), channel_id=1, source_target_pairs={{0,8},{8,16},{16,24},{24,0},{1,9},{9,17},{17,25},{25,1},{2,10},{10... | collective-permute-start | bytes 393224 | tf_op jit(solution)/shard_map/ppermute | solution.py:21
  108.5 8.7 %collective-permute-start.31 = (f32[2,16,1024]{2,1,0:T(8,128)S(1)}, f32[2,16,1024]{2,1,0:T(8,128)S(1)}, u32[]{:S(2)}, u32[]{:S(2)}) collective-permute-start(f32[2,16,1024]{2,1,0:T(8,128)S(1)} %get-tuple-element.15), channel_id=1, source_target_pairs={{0,24},{8,0},{16,8},{24,16},{1,25},{9,1},{17,9},{25,17},{2,26},{10... | collective-permute-start | bytes 393224 | tf_op jit(solution)/shard_map/ppermute | solution.py:21
  111.3 7.7 %collective-permute-start.32 = (f32[2,16,1024]{2,1,0:T(8,128)S(1)}, f32[2,16,1024]{2,1,0:T(8,128)S(1)}, u32[]{:S(2)}, u32[]{:S(2)}) collective-permute-start(f32[2,16,1024]{2,1,0:T(8,128)S(1)} %get-tuple-element.14), channel_id=1, source_target_pairs={{0,16},{8,24},{16,0},{24,8},{1,17},{9,25},{17,1},{25,9},{2,18},{10... | collective-permute-start | bytes 393224 | tf_op jit(solution)/shard_map/ppermute | solution.py:21
  119.0 4.8 %collective-permute-start.33 = (f32[16,1024]{1,0:T(8,128)S(1)}, f32[16,1024]{1,0:T(8,128)S(1)}, u32[]{:S(2)}, u32[]{:S(2)}) collective-permute-start(f32[16,1024]{1,0:T(8,128)S(1)} %get-tuple-element.16), channel_id=1, source_target_pairs={{0,64},{64,0},{1,65},{65,1},{2,66},{66,2},{3,67},{67,3},{4,68},{68... | collective-permute-start | bytes 196616 | tf_op jit(solution)/shard_map/ppermute | solution.py:21
  120.2 6.6 %collective-permute-start.34 = (f32[16,1024]{1,0:T(8,128)S(1)}, f32[16,1024]{1,0:T(8,128)S(1)}, u32[]{:S(2)}, u32[]{:S(2)}) collective-permute-start(f32[16,1024]{1,0:T(8,128)S(1)} %get-tuple-element.18), channel_id=1, source_target_pairs={{0,32},{32,0},{1,33},{33,1},{2,34},{34,2},{3,35},{35,3},{4,36},{36... | collective-permute-start | bytes 196616 | tf_op jit(solution)/shard_map/ppermute | solution.py:21
  123.8 5.5 %collective-permute-start.35 = (f32[16,1024]{1,0:T(8,128)S(1)}, f32[16,1024]{1,0:T(8,128)S(1)}, u32[]{:S(2)}, u32[]{:S(2)}) collective-permute-start(f32[16,1024]{1,0:T(8,128)S(1)} %get-tuple-element.17), channel_id=1, source_target_pairs={{0,96},{96,0},{32,64},{64,32},{1,97},{97,1},{33,65},{65,33},{2,98}... | collective-permute-start | bytes 196616 | tf_op jit(solution)/shard_map/ppermute | solution.py:25

commit v2 on v1

--- a/solution.py
+++ b/solution.py
@@ -214,7 +214,7 @@
         return lax.dynamic_index_in_dim(coef, lax.rem(y + k, 4), 1, keepdims=False)
 
     col = for_y(0)
-    for k in (1, 3, 2):
+    for k in (2, 1, 3):
         col = col + shift(for_y(k), "y", k)
 
     def weighted(f, z):
@@ -240,7 +240,9 @@
     s_block = assemble(s_pieces)
     r_pieces = both_cores(gather_points_yz(basis))
     greens = both_cores(gather_green_x(green))
-    chunks = [project(v, s_block) for v in greens]
+    chunks = []
+    for v in greens:
+        chunks.append(project(v, s_block))
     parts = main(chunks, r_pieces, s_block.shape[0])
     coef = jnp.dot(sum_over_x(parts), s_block, preferred_element_type=F32)
     return reduce_out(coef, time_weights)

time: 130 us -> 130 us (level)
  waiting for transfers between devices: 51.6 us -> 50.2 us
    ppermute x33, waiting for transfers between devices: 49.1 us -> 47.7 us  [shift(): return lax.ppermute(v, axis, [(i, (i + step) % n) for i in range(n)])]
where the time goes in v2:
time: 130 us; the launch traced here: 129 us
  waiting for transfers between devices  50.2 us (39%)
  starting transfers between devices  47.4 us (36%)
  Pallas kernels  19 us (15%)
  matrix products  5.51 us (4%)
  other arithmetic  3.78 us (3%)
  local copies, waits for them, and re-layouts  1.81 us (1%)
  between operations  1.55 us (1%)
    ppermute x33, waiting for transfers between devices, shift(): return lax.ppermute(v, axis, [(i, (i + step) % n) for i in range(n)])  47.7 us
    ppermute x33, starting transfers between devices, shift(): return lax.ppermute(v, axis, [(i, (i + step) % n) for i in range(n)])  43.4 us
    pallas_call x1, Pallas kernels, main(): pl.pallas_call(kernel, out_shape=[jax.ShapeDtypeStruct((8, 32, s_rows), B...  17.9 us
    dot_general x8, matrix products, nt(): lax.dot_general(a, b, (((1,), (1,)), ((), ())), preferred_element_type=F32)  4.94 us
    ppermute x3, starting transfers between devices, far_z(): return lax.ppermute(v, ('tm', 'zh'), [(0, 3), (3, 0), (1, 2), (2, 1)])  3.95 us
  transfers between devices with their start and end apart: 36, of which 17 were waited for; matrix products, arithmetic and copies ran while one was open for 6% of the time, Pallas kernels for 1%

profile of v2, /device:TPU:0, one launch (start us, length us, event | category | flops | bytes accessed | tf_op | source)
XLA Modules:
  0.0 129.3 jit_solution(15243038645244754552)
XLA Ops:
  0.0 0.8 pad_maximum_fusion.2
  0.8 4.1 %collective-permute-start = (bf16[2,16,1024]{2,1,0:T(8,128)(2,1)S(1)}, bf16[2,16,1024]{2,1,0:T(8,128)(2,1)S(1)}, u32[]{:S(2)}, u32[]{:S(2)}) collective-permute-start(bf16[2,16,1024]{2,1,0:T(8,128)(2,1)S(1)} %pad_maximum_fusion.2), channel_id=1, source_target_pairs={{0,32},{32,0},{1,33},{33,1},{2,34},{34,2},{3,35},{35,3},{4,36},{36... | collective-permute-start | bytes 196616 | tf_op jit(solution)/shard_map/ppermute | solution.py:21
  4.9 1.5 %collective-permute-start.4 = (bf16[192,1024]{1,0:T(8,128)(2,1)}, bf16[192,1024]{1,0:T(8,128)(2,1)S(1)}, u32[]{:S(2)}, u32[]{:S(2)}) collective-permute-start(bf16[192,1024]{1,0:T(8,128)(2,1)} %refs_0_.1), channel_id=1, source_target_pairs={{0,2},{2,4},{4,6},{6,0},{1,3},{3,5},{5,7},{7,1},{8,10},{10,12},{12... | collective-permute-start | bytes 1179656 | tf_op jit(solution)/shard_map/ppermute | solution.py:21
  6.4 1.7 %collective-permute-start.5 = (bf16[192,1024]{1,0:T(8,128)(2,1)}, bf16[192,1024]{1,0:T(8,128)(2,1)S(1)}, u32[]{:S(2)}, u32[]{:S(2)}) collective-permute-start(bf16[192,1024]{1,0:T(8,128)(2,1)} %refs_0_.1), channel_id=1, source_target_pairs={{0,6},{2,0},{4,2},{6,4},{1,7},{3,1},{5,3},{7,5},{8,14},{10,8},{12,... | collective-permute-start | bytes 1179656 | tf_op jit(solution)/shard_map/ppermute | solution.py:21
  8.1 0.7 collective-permute-start.16
  8.8 0.8 select_bitcast_fusion.1
  9.7 3.1 %collective-permute-start.1 = (bf16[2,2,16,1024]{3,2,1,0:T(8,128)(2,1)S(1)}, bf16[2,2,16,1024]{3,2,1,0:T(8,128)(2,1)S(1)}, u32[]{:S(2)}, u32[]{:S(2)}) collective-permute-start(bf16[2,2,16,1024]{3,2,1,0:T(8,128)(2,1)S(1)} %pad_maximum_fusion.1), channel_id=1, source_target_pairs={{0,24},{8,0},{16,8},{24,16},{1,25},{9,1},{17,9},{25,17},{2,26},{10... | collective-permute-start | bytes 393224 | tf_op jit(solution)/shard_map/ppermute | solution.py:21
  12.7 0.9 constant_dynamic-slice_fusion
  13.7 1.9 %collective-permute-start.6 = (bf16[96,1024]{1,0:T(8,128)(2,1)S(1)}, bf16[96,1024]{1,0:T(8,128)(2,1)S(1)}, u32[]{:S(2)}, u32[]{:S(2)}) collective-permute-start(bf16[96,1024]{1,0:T(8,128)(2,1)S(1)} %constant_dynamic-slice_fusion), channel_id=1, source_target_pairs={{0,4},{2,6},{4,0},{6,2},{1,5},{3,7},{5,1},{7,3},{8,12},{10,14},{12... | collective-permute-start | bytes 589832 | tf_op jit(solution)/shard_map/ppermute | solution.py:21
  15.7 2.2 %collective-permute-start.2 = (bf16[2,2,16,1024]{3,2,1,0:T(8,128)(2,1)S(1)}, bf16[2,2,16,1024]{3,2,1,0:T(8,128)(2,1)S(1)}, u32[]{:S(2)}, u32[]{:S(2)}) collective-permute-start(bf16[2,2,16,1024]{3,2,1,0:T(8,128)(2,1)S(1)} %pad_maximum_fusion.1), channel_id=1, source_target_pairs={{0,16},{8,24},{16,0},{24,8},{1,17},{9,25},{17,1},{25,9},{2,18},{10... | collective-permute-start | bytes 393224 | tf_op jit(solution)/shard_map/ppermute | solution.py:21
  17.9 4.3 %collective-permute-done.2 = bf16[2,2,16,1024]{3,2,1,0:T(8,128)(2,1)S(1)} collective-permute-done((bf16[2,2,16,1024]{3,2,1,0:T(8,128)(2,1)S(1)}, bf16[2,2,16,1024]{3,2,1,0:T(8,128)(2,1)S(1)}, u32[]{:S(2)}, u32[]{:S(2)}) %collective-permute-start.2) | collective-permute-done | bytes 131104 | tf_op jit(solution)/shard_map/ppermute | solution.py:21
  22.2 0.5 collective-permute-start.3
  22.8 5.6 %collective-permute-done.3 = bf16[2,2,16,1024]{3,2,1,0:T(8,128)(2,1)S(1)} collective-permute-done((bf16[2,2,16,1024]{3,2,1,0:T(8,128)(2,1)S(1)}, bf16[2,2,16,1024]{3,2,1,0:T(8,128)(2,1)S(1)}, u32[]{:S(2)}, u32[]{:S(2)}) %collective-permute-start.3) | collective-permute-done | bytes 131104 | tf_op jit(solution)/shard_map/ppermute | solution.py:21
  28.4 0.7 collective-permute-start.8
  29.1 1.1 collective-permute-start.7
  30.2 1.2 collective-permute-start.17
  31.4 3.4 %collective-permute-done.7.refs_4_ = bf16[96,1024]{1,0:T(8,128)(2,1)S(1)} collective-permute-done((bf16[96,1024]{1,0:T(8,128)(2,1)S(1)}, bf16[96,1024]{1,0:T(8,128)(2,1)S(1)}, u32[]{:S(2)}, u32[]{:S(2)}) %collective-permute-start.7) | collective-permute-done | bytes 196640 | tf_op jit(solution)/shard_map/ppermute | solution.py:21
  34.8 2.6 %collective-permute-start.9 = (bf16[2,8,16,1024]{3,2,1,0:T(8,128)(2,1)S(1)}, bf16[2,8,16,1024]{3,2,1,0:T(8,128)(2,1)S(1)}, u32[]{:S(2)}, u32[]{:S(2)}) collective-permute-start(bf16[2,8,16,1024]{3,2,1,0:T(8,128)(2,1)S(1)} %bitcast.112), channel_id=1, source_target_pairs={{0,6},{2,0},{4,2},{6,4},{1,7},{3,1},{5,3},{7,5},{8,14},{10,8},{12,... | collective-permute-start | bytes 1572872 | tf_op jit(solution)/shard_map/ppermute | solution.py:21
  37.4 0.1 collective-permute-start.18
  37.5 1.1 assemble.1
  38.6 0.6 convolution_convert_fusion.7
  39.3 0.3 collective-permute-done.17.refs_9_
  39.6 3.0 %collective-permute-start.20 = (bf16[384,1024]{1,0:T(8,128)(2,1)S(1)}, bf16[384,1024]{1,0:T(8,128)(2,1)S(1)}, u32[]{:S(2)}, u32[]{:S(2)}) collective-permute-start(bf16[384,1024]{1,0:T(8,128)(2,1)S(1)} %constant_dynamic-update-slice_fusion.refs_8_), channel_id=1, source_target_pairs={{0,24},{8,0},{16,8},{24,16},{1,25},{9,1},{17,9},{25,17},{2,26},{10... | collective-permute-start | bytes 2359304 | tf_op jit(solution)/shard_map/ppermute | solution.py:21
  42.5 3.2 %collective-permute-start.19 = (bf16[192,1024]{1,0:T(8,128)(2,1)S(1)}, bf16[192,1024]{1,0:T(8,128)(2,1)S(1)}, u32[]{:S(2)}, u32[]{:S(2)}) collective-permute-start(bf16[192,1024]{1,0:T(8,128)(2,1)S(1)} %collective-permute-done.17.refs_9_), channel_id=1, source_target_pairs={{0,96},{96,0},{32,64},{64,32},{1,97},{97,1},{33,65},{65,33},{2,98}... | collective-permute-start | bytes 1179656 | tf_op jit(solution)/shard_map/ppermute | solution.py:25
  45.9 0.6 convolution_convert_fusion.5
  46.5 3.3 %collective-permute-start.11 = (bf16[8,16,1024]{2,1,0:T(8,128)(2,1)S(1)}, bf16[8,16,1024]{2,1,0:T(8,128)(2,1)S(1)}, u32[]{:S(2)}, u32[]{:S(2)}) collective-permute-start(bf16[8,16,1024]{2,1,0:T(8,128)(2,1)S(1)} %slice_bitcast_fusion), channel_id=1, source_target_pairs={{0,6},{2,0},{4,2},{6,4},{1,7},{3,1},{5,3},{7,5},{8,14},{10,8},{12,... | collective-permute-start | bytes 786440 | tf_op jit(solution)/shard_map/ppermute | solution.py:21
  49.8 0.6 convolution_convert_fusion.3
  50.4 4.4 %collective-permute-done.10 = bf16[8,16,1024]{2,1,0:T(8,128)(2,1)S(1)} collective-permute-done((bf16[8,16,1024]{2,1,0:T(8,128)(2,1)S(1)}, bf16[8,16,1024]{2,1,0:T(8,128)(2,1)S(1)}, u32[]{:S(2)}, u32[]{:S(2)}) %collective-permute-start.10) | collective-permute-done | bytes 262176 | tf_op jit(solution)/shard_map/ppermute | solution.py:21
  54.9 0.6 convolution_convert_fusion.6
  55.5 0.6 collective-permute-start.14
  56.1 0.1 collective-permute-start.15
  56.2 0.6 convolution_convert_fusion.4
  56.9 1.7 %collective-permute-done.18.refs_10_ = bf16[384,1024]{1,0:T(8,128)(2,1)S(1)} collective-permute-done((bf16[384,1024]{1,0:T(8,128)(2,1)S(1)}, bf16[384,1024]{1,0:T(8,128)(2,1)S(1)}, u32[]{:S(2)}, u32[]{:S(2)}) %collective-permute-start.18) | collective-permute-done | bytes 786464 | tf_op jit(solution)/shard_map/ppermute | solution.py:21
  58.6 1.1 collective-permute-done.20.refs_12_
  59.7 0.5 collective-permute-start.25
  60.2 0.6 convolution_convert_fusion.2
  60.8 0.1 collective-permute-start.22
  60.9 0.5 collective-permute-start.24
  61.4 0.6 convolution_convert_fusion.1
  62.0 0.6 convolution_convert_fusion
  62.7 1.0 collective-permute-done.22.refs_14_
  63.7 0.6 collective-permute-done.24.refs_16_
  64.2 17.9 %main.1 = (bf16[8,32,768]{2,1,0:T(8,128)(2,1)S(1)}, bf16[8,32,768]{2,1,0:T(8,128)(2,1)S(1)}, bf16[8,32,768]{2,1,0:T(8,128)(2,1)S(1)}, bf16[8,32,768]{2,1,0:T(8,128)(2,1)S(1)}) custom-call(bf16[2,8,16,768]{3,2,1,0:T(8,128)(2,1)S(1)} %bitcast.101, bf16[2,8,16,768]{3,2,1,0:T(8,128)(2,1)S(1)} %bitcast.104, bf16[2,8,16,768]{3,2,1,0:T(8,128)(2,1)S(1)} %bitcast.102, ...), custom_call_target="tpu_custom_call" | custom-call | flops 14495514624 | bytes 12582912 | tf_op jit(solution)/shard_map/main/pallas_call | solution.py:129
  82.2 0.6 collective-permute-start.26
  82.8 1.8 %collective-permute-start.27 = (bf16[8,32,768]{2,1,0:T(8,128)(2,1)S(1)}, bf16[8,32,768]{2,1,0:T(8,128)(2,1)}, u32[]{:S(2)}, u32[]{:S(2)}) collective-permute-start(bf16[8,32,768]{2,1,0:T(8,128)(2,1)S(1)} %get-tuple-element.11), channel_id=1, source_target_pairs={{0,2},{2,4},{4,6},{6,0},{1,3},{3,5},{5,7},{7,1},{8,10},{10,12},{12... | collective-permute-start | bytes 1179656 | tf_op jit(solution)/shard_map/ppermute | solution.py:21
  84.6 1.4 %collective-permute-start.28 = (bf16[8,32,768]{2,1,0:T(8,128)(2,1)S(1)}, bf16[8,32,768]{2,1,0:T(8,128)(2,1)}, u32[]{:S(2)}, u32[]{:S(2)}) collective-permute-start(bf16[8,32,768]{2,1,0:T(8,128)(2,1)S(1)} %get-tuple-element.12), channel_id=1, source_target_pairs={{0,6},{2,0},{4,2},{6,4},{1,7},{3,1},{5,3},{7,5},{8,14},{10,8},{12,... | collective-permute-start | bytes 1179656 | tf_op jit(solution)/shard_map/ppermute | solution.py:21
  86.0 9.8 %collective-permute-done.26 = bf16[8,32,768]{2,1,0:T(8,128)(2,1)S(1)} collective-permute-done((bf16[8,32,768]{2,1,0:T(8,128)(2,1)S(1)}, bf16[8,32,768]{2,1,0:T(8,128)(2,1)S(1)}, u32[]{:S(2)}, u32[]{:S(2)}) %collective-permute-start.26) | collective-permute-done | bytes 393248 | tf_op jit(solution)/shard_map/ppermute | solution.py:21
  95.8 7.6 %collective-permute-done.27 = bf16[8,32,768]{2,1,0:T(8,128)(2,1)} collective-permute-done((bf16[8,32,768]{2,1,0:T(8,128)(2,1)S(1)}, bf16[8,32,768]{2,1,0:T(8,128)(2,1)}, u32[]{:S(2)}, u32[]{:S(2)}) %collective-permute-start.27) | collective-permute-done | bytes 393248 | tf_op jit(solution)/shard_map/ppermute | solution.py:21
  103.4 1.3 %add_convert_fusion = bf16[8,32,768]{2,1,0:T(8,128)(2,1)S(1)} fusion(bf16[8,32,768]{2,1,0:T(8,128)(2,1)} %collective-permute-done.28, bf16[8,32,768]{2,1,0:T(8,128)(2,1)} %collective-permute-done.27, bf16[8,32,768]{2,1,0:T(8,128)(2,1)S(1)} %collective-permute-done.26, bf16[8,32,768]{2,1,0:T(8,128)(2,1)S(1)} %get-tuple-element.9), kind=kLoop, calls=%fused_computation.10 | loop fusion | flops 1572864 | bytes 1966080 | tf_op jit(solution)/shard_map/convert_element_type | solution.py:199
  104.7 0.6 fusion
  105.4 0.1 collective-permute-start.29
  105.5 1.9 %collective-permute-done.29 = f32[8,16,1024]{2,1,0:T(8,128)S(1)} collective-permute-done((f32[8,16,1024]{2,1,0:T(8,128)S(1)}, f32[8,16,1024]{2,1,0:T(8,128)S(1)}, u32[]{:S(2)}, u32[]{:S(2)}) %collective-permute-start.29) | collective-permute-done | bytes 524320 | tf_op jit(solution)/shard_map/ppermute | solution.py:21
  107.5 2.8 %collective-permute-start.30 = (f32[2,16,1024]{2,1,0:T(8,128)S(1)}, f32[2,16,1024]{2,1,0:T(8,128)S(1)}, u32[]{:S(2)}, u32[]{:S(2)}) collective-permute-start(f32[2,16,1024]{2,1,0:T(8,128)S(1)} %get-tuple-element.13), channel_id=1, source_target_pairs={{0,16},{8,24},{16,0},{24,8},{1,17},{9,25},{17,1},{25,9},{2,18},{10... | collective-permute-start | bytes 393224 | tf_op jit(solution)/shard_map/ppermute | solution.py:21
  110.2 1.8 %collective-permute-start.31 = (f32[2,16,1024]{2,1,0:T(8,128)S(1)}, f32[2,16,1024]{2,1,0:T(8,128)S(1)}, u32[]{:S(2)}, u32[]{:S(2)}) collective-permute-start(f32[2,16,1024]{2,1,0:T(8,128)S(1)} %get-tuple-element.15), channel_id=1, source_target_pairs={{0,8},{8,16},{16,24},{24,0},{1,9},{9,17},{17,25},{25,1},{2,10},{10... | collective-permute-start | bytes 393224 | tf_op jit(solution)/shard_map/ppermute | solution.py:21
  112.1 1.4 %collective-permute-start.32 = (f32[2,16,1024]{2,1,0:T(8,128)S(1)}, f32[2,16,1024]{2,1,0:T(8,128)S(1)}, u32[]{:S(2)}, u32[]{:S(2)}) collective-permute-start(f32[2,16,1024]{2,1,0:T(8,128)S(1)} %get-tuple-element.14), channel_id=1, source_target_pairs={{0,24},{8,0},{16,8},{24,16},{1,25},{9,1},{17,9},{25,17},{2,26},{10... | collective-permute-start | bytes 393224 | tf_op jit(solution)/shard_map/ppermute | solution.py:21
  113.5 0.6 fusion.7
  115.3 0.1 collective-permute-done.30
  115.4 2.1 %collective-permute-done.31 = f32[2,16,1024]{2,1,0:T(8,128)S(1)} collective-permute-done((f32[2,16,1024]{2,1,0:T(8,128)S(1)}, f32[2,16,1024]{2,1,0:T(8,128)S(1)}, u32[]{:S(2)}, u32[]{:S(2)}) %collective-permute-start.31) | collective-permute-done | bytes 131104 | tf_op jit(solution)/shard_map/ppermute | solution.py:21
  117.5 0.9 collective-permute-done.32
  118.5 1.1 collective-permute-start.33
  119.6 3.6 %collective-permute-start.34 = (f32[16,1024]{1,0:T(8,128)S(1)}, f32[16,1024]{1,0:T(8,128)S(1)}, u32[]{:S(2)}, u32[]{:S(2)}) collective-permute-start(f32[16,1024]{1,0:T(8,128)S(1)} %get-tuple-element.18), channel_id=1, source_target_pairs={{0,32},{32,0},{1,33},{33,1},{2,34},{34,2},{3,35},{35,3},{4,36},{36... | collective-permute-start | bytes 196616 | tf_op jit(solution)/shard_map/ppermute | solution.py:21
  123.2 2.9 %collective-permute-done.34 = f32[16,1024]{1,0:T(8,128)S(1)} collective-permute-done((f32[16,1024]{1,0:T(8,128)S(1)}, f32[16,1024]{1,0:T(8,128)S(1)}, u32[]{:S(2)}, u32[]{:S(2)}) %collective-permute-start.34) | collective-permute-done | bytes 65568 | tf_op jit(solution)/shard_map/ppermute | solution.py:21
  126.2 2.5 %collective-permute-done.35 = f32[16,1024]{1,0:T(8,128)S(1)} collective-permute-done((f32[16,1024]{1,0:T(8,128)S(1)}, f32[16,1024]{1,0:T(8,128)S(1)}, u32[]{:S(2)}, u32[]{:S(2)}) %collective-permute-start.35) | collective-permute-done | bytes 65568 | tf_op jit(solution)/shard_map/ppermute | solution.py:25
  128.7 0.6 fusion.6
  (45 shorter events, 0.6 us)
Async XLA Ops:
  0.0 30.2 %copy-start = (bf16[192,1024]{1,0:T(8,128)(2,1)S(1)}, bf16[192,1024]{1,0:T(8,128)(2,1)}, u32[]{:S(2)}) copy-start(bf16[192,1024]{1,0:T(8,128)(2,1)} %refs_0_.1) | copy-start | bytes 1179652
  0.8 8.0 %collective-permute-start = (bf16[2,16,1024]{2,1,0:T(8,128)(2,1)S(1)}, bf16[2,16,1024]{2,1,0:T(8,128)(2,1)S(1)}, u32[]{:S(2)}, u32[]{:S(2)}) collective-permute-start(bf16[2,16,1024]{2,1,0:T(8,128)(2,1)S(1)} %pad_maximum_fusion.2), channel_id=1, source_target_pairs={{0,32},{32,0},{1,33},{33,1},{2,34},{34,2},{3,35},{35,3},{4,36},{36... | collective-permute-start | bytes 196616 | tf_op jit(solution)/shard_map/ppermute | solution.py:21
  4.9 32.5 %collective-permute-start.4 = (bf16[192,1024]{1,0:T(8,128)(2,1)}, bf16[192,1024]{1,0:T(8,128)(2,1)S(1)}, u32[]{:S(2)}, u32[]{:S(2)}) collective-permute-start(bf16[192,1024]{1,0:T(8,128)(2,1)} %refs_0_.1), channel_id=1, source_target_pairs={{0,2},{2,4},{4,6},{6,0},{1,3},{3,5},{5,7},{7,1},{8,10},{10,12},{12... | collective-permute-start | bytes 1179656 | tf_op jit(solution)/shard_map/ppermute | solution.py:21
  6.4 31.0 %collective-permute-start.5 = (bf16[192,1024]{1,0:T(8,128)(2,1)}, bf16[192,1024]{1,0:T(8,128)(2,1)S(1)}, u32[]{:S(2)}, u32[]{:S(2)}) collective-permute-start(bf16[192,1024]{1,0:T(8,128)(2,1)} %refs_0_.1), channel_id=1, source_target_pairs={{0,6},{2,0},{4,2},{6,4},{1,7},{3,1},{5,3},{7,5},{8,14},{10,8},{12,... | collective-permute-start | bytes 1179656 | tf_op jit(solution)/shard_map/ppermute | solution.py:21
  8.1 22.1 %collective-permute-start.16 = (bf16[192,1024]{1,0:T(8,128)(2,1)}, bf16[192,1024]{1,0:T(8,128)(2,1)S(1)}, u32[]{:S(2)}, u32[]{:S(2)}) collective-permute-start(bf16[192,1024]{1,0:T(8,128)(2,1)} %refs_0_.1), channel_id=1, source_target_pairs={{0,96},{96,0},{32,64},{64,32},{1,97},{97,1},{33,65},{65,33},{2,98}... | collective-permute-start | bytes 1179656 | tf_op jit(solution)/shard_map/ppermute | solution.py:25
  9.7 6.0 %collective-permute-start.1 = (bf16[2,2,16,1024]{3,2,1,0:T(8,128)(2,1)S(1)}, bf16[2,2,16,1024]{3,2,1,0:T(8,128)(2,1)S(1)}, u32[]{:S(2)}, u32[]{:S(2)}) collective-permute-start(bf16[2,2,16,1024]{3,2,1,0:T(8,128)(2,1)S(1)} %pad_maximum_fusion.1), channel_id=1, source_target_pairs={{0,24},{8,0},{16,8},{24,16},{1,25},{9,1},{17,9},{25,17},{2,26},{10... | collective-permute-start | bytes 393224 | tf_op jit(solution)/shard_map/ppermute | solution.py:21
  13.7 15.4 %collective-permute-start.6 = (bf16[96,1024]{1,0:T(8,128)(2,1)S(1)}, bf16[96,1024]{1,0:T(8,128)(2,1)S(1)}, u32[]{:S(2)}, u32[]{:S(2)}) collective-permute-start(bf16[96,1024]{1,0:T(8,128)(2,1)S(1)} %constant_dynamic-slice_fusion), channel_id=1, source_target_pairs={{0,4},{2,6},{4,0},{6,2},{1,5},{3,7},{5,1},{7,3},{8,12},{10,14},{12... | collective-permute-start | bytes 589832 | tf_op jit(solution)/shard_map/ppermute | solution.py:21
  15.7 6.6 %collective-permute-start.2 = (bf16[2,2,16,1024]{3,2,1,0:T(8,128)(2,1)S(1)}, bf16[2,2,16,1024]{3,2,1,0:T(8,128)(2,1)S(1)}, u32[]{:S(2)}, u32[]{:S(2)}) collective-permute-start(bf16[2,2,16,1024]{3,2,1,0:T(8,128)(2,1)S(1)} %pad_maximum_fusion.1), channel_id=1, source_target_pairs={{0,16},{8,24},{16,0},{24,8},{1,17},{9,25},{17,1},{25,9},{2,18},{10... | collective-permute-start | bytes 393224 | tf_op jit(solution)/shard_map/ppermute | solution.py:21
  22.2 6.2 %collective-permute-start.3 = (bf16[2,2,16,1024]{3,2,1,0:T(8,128)(2,1)S(1)}, bf16[2,2,16,1024]{3,2,1,0:T(8,128)(2,1)S(1)}, u32[]{:S(2)}, u32[]{:S(2)}) collective-permute-start(bf16[2,2,16,1024]{3,2,1,0:T(8,128)(2,1)S(1)} %pad_maximum_fusion.1), channel_id=1, source_target_pairs={{0,8},{8,16},{16,24},{24,0},{1,9},{9,17},{17,25},{25,1},{2,10},{10... | collective-permute-start | bytes 393224 | tf_op jit(solution)/shard_map/ppermute | solution.py:21
  28.4 14.1 %collective-permute-start.8 = (bf16[2,8,16,1024]{3,2,1,0:T(8,128)(2,1)S(1)}, bf16[2,8,16,1024]{3,2,1,0:T(8,128)(2,1)S(1)}, u32[]{:S(2)}, u32[]{:S(2)}) collective-permute-start(bf16[2,8,16,1024]{3,2,1,0:T(8,128)(2,1)S(1)} %bitcast.111), channel_id=1, source_target_pairs={{0,2},{2,4},{4,6},{6,0},{1,3},{3,5},{5,7},{7,1},{8,10},{10,12},{12... | collective-permute-start | bytes 1572872 | tf_op jit(solution)/shard_map/ppermute | solution.py:21
  29.1 5.7 %collective-permute-start.7 = (bf16[96,1024]{1,0:T(8,128)(2,1)S(1)}, bf16[96,1024]{1,0:T(8,128)(2,1)S(1)}, u32[]{:S(2)}, u32[]{:S(2)}) collective-permute-start(bf16[96,1024]{1,0:T(8,128)(2,1)S(1)} %collective-permute-done.6.refs_3_), channel_id=1, source_target_pairs={{0,64},{64,0},{1,65},{65,1},{2,66},{66,2},{3,67},{67,3},{4,68},{68... | collective-permute-start | bytes 589832 | tf_op jit(solution)/shard_map/ppermute | solution.py:21
  30.2 9.4 %collective-permute-start.17 = (bf16[192,1024]{1,0:T(8,128)(2,1)S(1)}, bf16[192,1024]{1,0:T(8,128)(2,1)S(1)}, u32[]{:S(2)}, u32[]{:S(2)}) collective-permute-start(bf16[192,1024]{1,0:T(8,128)(2,1)S(1)} %copy-done), channel_id=1, source_target_pairs={{0,16},{8,24},{16,0},{24,8},{1,17},{9,25},{17,1},{25,9},{2,18},{10... | collective-permute-start | bytes 1179656 | tf_op jit(solution)/shard_map/ppermute | solution.py:21
  34.8 11.0 %collective-permute-start.9 = (bf16[2,8,16,1024]{3,2,1,0:T(8,128)(2,1)S(1)}, bf16[2,8,16,1024]{3,2,1,0:T(8,128)(2,1)S(1)}, u32[]{:S(2)}, u32[]{:S(2)}) collective-permute-start(bf16[2,8,16,1024]{3,2,1,0:T(8,128)(2,1)S(1)} %bitcast.112), channel_id=1, source_target_pairs={{0,6},{2,0},{4,2},{6,4},{1,7},{3,1},{5,3},{7,5},{8,14},{10,8},{12,... | collective-permute-start | bytes 1572872 | tf_op jit(solution)/shard_map/ppermute | solution.py:21
  37.4 9.1 %collective-permute-start.12 = (bf16[2,8,16,1024]{3,2,1,0:T(8,128)(2,1)S(1)}, bf16[2,8,16,1024]{3,2,1,0:T(8,128)(2,1)S(1)}, u32[]{:S(2)}, u32[]{:S(2)}) collective-permute-start(bf16[2,8,16,1024]{3,2,1,0:T(8,128)(2,1)S(1)} %bitcast.113), channel_id=1, source_target_pairs={{0,1},{1,0},{2,3},{3,2},{4,5},{5,4},{6,7},{7,6},{8,9},{9,8},{10,11... | collective-permute-start | bytes 1572872 | tf_op jit(solution)/shard_map/ppermute | solution.py:21
  37.4 21.2 %collective-permute-start.18 = (bf16[384,1024]{1,0:T(8,128)(2,1)S(1)}, bf16[384,1024]{1,0:T(8,128)(2,1)S(1)}, u32[]{:S(2)}, u32[]{:S(2)}) collective-permute-start(bf16[384,1024]{1,0:T(8,128)(2,1)S(1)} %constant_dynamic-update-slice_fusion.refs_8_), channel_id=1, source_target_pairs={{0,8},{8,16},{16,24},{24,0},{1,9},{9,17},{17,25},{25,1},{2,10},{10... | collective-permute-start | bytes 2359304 | tf_op jit(solution)/shard_map/ppermute | solution.py:21
  39.6 20.1 %collective-permute-start.20 = (bf16[384,1024]{1,0:T(8,128)(2,1)S(1)}, bf16[384,1024]{1,0:T(8,128)(2,1)S(1)}, u32[]{:S(2)}, u32[]{:S(2)}) collective-permute-start(bf16[384,1024]{1,0:T(8,128)(2,1)S(1)} %constant_dynamic-update-slice_fusion.refs_8_), channel_id=1, source_target_pairs={{0,24},{8,0},{16,8},{24,16},{1,25},{9,1},{17,9},{25,17},{2,26},{10... | collective-permute-start | bytes 2359304 | tf_op jit(solution)/shard_map/ppermute | solution.py:21
  42.5 13.6 %collective-permute-start.19 = (bf16[192,1024]{1,0:T(8,128)(2,1)S(1)}, bf16[192,1024]{1,0:T(8,128)(2,1)S(1)}, u32[]{:S(2)}, u32[]{:S(2)}) collective-permute-start(bf16[192,1024]{1,0:T(8,128)(2,1)S(1)} %collective-permute-done.17.refs_9_), channel_id=1, source_target_pairs={{0,96},{96,0},{32,64},{64,32},{1,97},{97,1},{33,65},{65,33},{2,98}... | collective-permute-start | bytes 1179656 | tf_op jit(solution)/shard_map/ppermute | solution.py:25
  45.8 9.1 %collective-permute-start.10 = (bf16[8,16,1024]{2,1,0:T(8,128)(2,1)S(1)}, bf16[8,16,1024]{2,1,0:T(8,128)(2,1)S(1)}, u32[]{:S(2)}, u32[]{:S(2)}) collective-permute-start(bf16[8,16,1024]{2,1,0:T(8,128)(2,1)S(1)} %slice_bitcast_fusion.1), channel_id=1, source_target_pairs={{0,2},{2,4},{4,6},{6,0},{1,3},{3,5},{5,7},{7,1},{8,10},{10,12},{12... | collective-permute-start | bytes 786440 | tf_op jit(solution)/shard_map/ppermute | solution.py:21
  46.5 9.0 %collective-permute-start.11 = (bf16[8,16,1024]{2,1,0:T(8,128)(2,1)S(1)}, bf16[8,16,1024]{2,1,0:T(8,128)(2,1)S(1)}, u32[]{:S(2)}, u32[]{:S(2)}) collective-permute-start(bf16[8,16,1024]{2,1,0:T(8,128)(2,1)S(1)} %slice_bitcast_fusion), channel_id=1, source_target_pairs={{0,6},{2,0},{4,2},{6,4},{1,7},{3,1},{5,3},{7,5},{8,14},{10,8},{12,... | collective-permute-start | bytes 786440 | tf_op jit(solution)/shard_map/ppermute | solution.py:21
  54.9 4.8 %collective-permute-start.13 = (bf16[2,8,16,1024]{3,2,1,0:T(8,128)(2,1)S(1)}, bf16[2,8,16,1024]{3,2,1,0:T(8,128)(2,1)S(1)}, u32[]{:S(2)}, u32[]{:S(2)}) collective-permute-start(bf16[2,8,16,1024]{3,2,1,0:T(8,128)(2,1)S(1)} %collective-permute-done.8), channel_id=1, source_target_pairs={{0,1},{1,0},{2,3},{3,2},{4,5},{5,4},{6,7},{7,6},{8,9},{9,8},{10,11... | collective-permute-start | bytes 1572872 | tf_op jit(solution)/shard_map/ppermute | solution.py:21
  55.5 5.3 %collective-permute-start.14 = (bf16[2,8,16,1024]{3,2,1,0:T(8,128)(2,1)S(1)}, bf16[2,8,16,1024]{3,2,1,0:T(8,128)(2,1)S(1)}, u32[]{:S(2)}, u32[]{:S(2)}) collective-permute-start(bf16[2,8,16,1024]{3,2,1,0:T(8,128)(2,1)S(1)} %collective-permute-done.9), channel_id=1, source_target_pairs={{0,1},{1,0},{2,3},{3,2},{4,5},{5,4},{6,7},{7,6},{8,9},{9,8},{10,11... | collective-permute-start | bytes 1572872 | tf_op jit(solution)/shard_map/ppermute | solution.py:21
  56.1 4.8 %collective-permute-start.15 = (bf16[2,8,16,1024]{3,2,1,0:T(8,128)(2,1)S(1)}, bf16[2,8,16,1024]{3,2,1,0:T(8,128)(2,1)S(1)}, u32[]{:S(2)}, u32[]{:S(2)}) collective-permute-start(bf16[2,8,16,1024]{3,2,1,0:T(8,128)(2,1)S(1)} %pad_maximum_fusion), channel_id=1, source_target_pairs={{0,1},{1,0},{2,3},{3,2},{4,5},{5,4},{6,7},{7,6},{8,9},{9,8},{10,11... | collective-permute-start | bytes 1572872 | tf_op jit(solution)/shard_map/ppermute | solution.py:21
  58.6 5.1 %collective-permute-start.21 = (bf16[384,1024]{1,0:T(8,128)(2,1)S(1)}, bf16[384,1024]{1,0:T(8,128)(2,1)S(1)}, u32[]{:S(2)}, u32[]{:S(2)}) collective-permute-start(bf16[384,1024]{1,0:T(8,128)(2,1)S(1)} %constant_dynamic-update-slice_fusion.refs_8_), channel_id=1, source_target_pairs={{0,1},{1,0},{2,3},{3,2},{4,5},{5,4},{6,7},{7,6},{8,9},{9,8},{10,11... | collective-permute-start | bytes 2359304 | tf_op jit(solution)/shard_map/ppermute | solution.py:21
  59.7 4.6 %collective-permute-start.23 = (bf16[384,1024]{1,0:T(8,128)(2,1)S(1)}, bf16[384,1024]{1,0:T(8,128)(2,1)S(1)}, u32[]{:S(2)}, u32[]{:S(2)}) collective-permute-start(bf16[384,1024]{1,0:T(8,128)(2,1)S(1)} %collective-permute-done.18.refs_10_), channel_id=1, source_target_pairs={{0,1},{1,0},{2,3},{3,2},{4,5},{5,4},{6,7},{7,6},{8,9},{9,8},{10,11... | collective-permute-start | bytes 2359304 | tf_op jit(solution)/shard_map/ppermute | solution.py:21
  59.7 4.6 %collective-permute-start.25 = (bf16[384,1024]{1,0:T(8,128)(2,1)S(1)}, bf16[384,1024]{1,0:T(8,128)(2,1)S(1)}, u32[]{:S(2)}, u32[]{:S(2)}) collective-permute-start(bf16[384,1024]{1,0:T(8,128)(2,1)S(1)} %collective-permute-done.20.refs_12_), channel_id=1, source_target_pairs={{0,1},{1,0},{2,3},{3,2},{4,5},{5,4},{6,7},{7,6},{8,9},{9,8},{10,11... | collective-permute-start | bytes 2359304 | tf_op jit(solution)/shard_map/ppermute | solution.py:21
  60.8 2.8 %collective-permute-start.22 = (bf16[192,1024]{1,0:T(8,128)(2,1)S(1)}, bf16[192,1024]{1,0:T(8,128)(2,1)S(1)}, u32[]{:S(2)}, u32[]{:S(2)}) collective-permute-start(bf16[192,1024]{1,0:T(8,128)(2,1)S(1)} %collective-permute-done.17.refs_9_), channel_id=1, source_target_pairs={{0,1},{1,0},{2,3},{3,2},{4,5},{5,4},{6,7},{7,6},{8,9},{9,8},{10,11... | collective-permute-start | bytes 1179656 | tf_op jit(solution)/shard_map/ppermute | solution.py:21
  60.9 3.3 %collective-permute-start.24 = (bf16[192,1024]{1,0:T(8,128)(2,1)S(1)}, bf16[192,1024]{1,0:T(8,128)(2,1)S(1)}, u32[]{:S(2)}, u32[]{:S(2)}) collective-permute-start(bf16[192,1024]{1,0:T(8,128)(2,1)S(1)} %collective-permute-done.19.refs_11_), channel_id=1, source_target_pairs={{0,1},{1,0},{2,3},{3,2},{4,5},{5,4},{6,7},{7,6},{8,9},{9,8},{10,11... | collective-permute-start | bytes 1179656 | tf_op jit(solution)/shard_map/ppermute | solution.py:21
  82.2 13.6 %collective-permute-start.26 = (bf16[8,32,768]{2,1,0:T(8,128)(2,1)S(1)}, bf16[8,32,768]{2,1,0:T(8,128)(2,1)S(1)}, u32[]{:S(2)}, u32[]{:S(2)}) collective-permute-start(bf16[8,32,768]{2,1,0:T(8,128)(2,1)S(1)} %get-tuple-element.10), channel_id=1, source_target_pairs={{0,4},{2,6},{4,0},{6,2},{1,5},{3,7},{5,1},{7,3},{8,12},{10,14},{12... | collective-permute-start | bytes 1179656 | tf_op jit(solution)/shard_map/ppermute | solution.py:21
  82.8 20.6 %collective-permute-start.27 = (bf16[8,32,768]{2,1,0:T(8,128)(2,1)S(1)}, bf16[8,32,768]{2,1,0:T(8,128)(2,1)}, u32[]{:S(2)}, u32[]{:S(2)}) collective-permute-start(bf16[8,32,768]{2,1,0:T(8,128)(2,1)S(1)} %get-tuple-element.11), channel_id=1, source_target_pairs={{0,2},{2,4},{4,6},{6,0},{1,3},{3,5},{5,7},{7,1},{8,10},{10,12},{12... | collective-permute-start | bytes 1179656 | tf_op jit(solution)/shard_map/ppermute | solution.py:21
  84.6 18.8 %collective-permute-start.28 = (bf16[8,32,768]{2,1,0:T(8,128)(2,1)S(1)}, bf16[8,32,768]{2,1,0:T(8,128)(2,1)}, u32[]{:S(2)}, u32[]{:S(2)}) collective-permute-start(bf16[8,32,768]{2,1,0:T(8,128)(2,1)S(1)} %get-tuple-element.12), channel_id=1, source_target_pairs={{0,6},{2,0},{4,2},{6,4},{1,7},{3,1},{5,3},{7,5},{8,14},{10,8},{12,... | collective-permute-start | bytes 1179656 | tf_op jit(solution)/shard_map/ppermute | solution.py:21
  105.3 8.2 %copy-start.1 = (f32[2,2]{1,0:T(2,128)S(1)}, f32[2,2]{1,0:T(2,128)}, u32[]{:S(2)}) copy-start(f32[2,2]{1,0:T(2,128)} %param.7) | copy-start | bytes 52
  105.4 2.0 %collective-permute-start.29 = (f32[8,16,1024]{2,1,0:T(8,128)S(1)}, f32[8,16,1024]{2,1,0:T(8,128)S(1)}, u32[]{:S(2)}, u32[]{:S(2)}) collective-permute-start(f32[8,16,1024]{2,1,0:T(8,128)S(1)} %dynamic-slice_bitcast_fusion), channel_id=1, source_target_pairs={{0,1},{1,0},{2,3},{3,2},{4,5},{5,4},{6,7},{7,6},{8,9},{9,8},{10,11... | collective-permute-start | bytes 1572872 | tf_op jit(solution)/shard_map/ppermute | solution.py:21
  107.5 8.0 %collective-permute-start.30 = (f32[2,16,1024]{2,1,0:T(8,128)S(1)}, f32[2,16,1024]{2,1,0:T(8,128)S(1)}, u32[]{:S(2)}, u32[]{:S(2)}) collective-permute-start(f32[2,16,1024]{2,1,0:T(8,128)S(1)} %get-tuple-element.13), channel_id=1, source_target_pairs={{0,16},{8,24},{16,0},{24,8},{1,17},{9,25},{17,1},{25,9},{2,18},{10... | collective-permute-start | bytes 393224 | tf_op jit(solution)/shard_map/ppermute | solution.py:21
  110.2 7.2 %collective-permute-start.31 = (f32[2,16,1024]{2,1,0:T(8,128)S(1)}, f32[2,16,1024]{2,1,0:T(8,128)S(1)}, u32[]{:S(2)}, u32[]{:S(2)}) collective-permute-start(f32[2,16,1024]{2,1,0:T(8,128)S(1)} %get-tuple-element.15), channel_id=1, source_target_pairs={{0,8},{8,16},{16,24},{24,0},{1,9},{9,17},{17,25},{25,1},{2,10},{10... | collective-permute-start | bytes 393224 | tf_op jit(solution)/shard_map/ppermute | solution.py:21
  112.1 6.3 %collective-permute-start.32 = (f32[2,16,1024]{2,1,0:T(8,128)S(1)}, f32[2,16,1024]{2,1,0:T(8,128)S(1)}, u32[]{:S(2)}, u32[]{:S(2)}) collective-permute-start(f32[2,16,1024]{2,1,0:T(8,128)S(1)} %get-tuple-element.14), channel_id=1, source_target_pairs={{0,24},{8,0},{16,8},{24,16},{1,25},{9,1},{17,9},{25,17},{2,26},{10... | collective-permute-start | bytes 393224 | tf_op jit(solution)/shard_map/ppermute | solution.py:21
  118.5 4.8 %collective-permute-start.33 = (f32[16,1024]{1,0:T(8,128)S(1)}, f32[16,1024]{1,0:T(8,128)S(1)}, u32[]{:S(2)}, u32[]{:S(2)}) collective-permute-start(f32[16,1024]{1,0:T(8,128)S(1)} %get-tuple-element.16), channel_id=1, source_target_pairs={{0,64},{64,0},{1,65},{65,1},{2,66},{66,2},{3,67},{67,3},{4,68},{68... | collective-permute-start | bytes 196616 | tf_op jit(solution)/shard_map/ppermute | solution.py:21
  119.6 6.6 %collective-permute-start.34 = (f32[16,1024]{1,0:T(8,128)S(1)}, f32[16,1024]{1,0:T(8,128)S(1)}, u32[]{:S(2)}, u32[]{:S(2)}) collective-permute-start(f32[16,1024]{1,0:T(8,128)S(1)} %get-tuple-element.18), channel_id=1, source_target_pairs={{0,32},{32,0},{1,33},{33,1},{2,34},{34,2},{3,35},{35,3},{4,36},{36... | collective-permute-start | bytes 196616 | tf_op jit(solution)/shard_map/ppermute | solution.py:21
  123.2 5.5 %collective-permute-start.35 = (f32[16,1024]{1,0:T(8,128)S(1)}, f32[16,1024]{1,0:T(8,128)S(1)}, u32[]{:S(2)}, u32[]{:S(2)}) collective-permute-start(f32[16,1024]{1,0:T(8,128)S(1)} %get-tuple-element.17), channel_id=1, source_target_pairs={{0,96},{96,0},{32,64},{64,32},{1,97},{97,1},{33,65},{65,33},{2,98}... | collective-permute-start | bytes 196616 | tf_op jit(solution)/shard_map/ppermute | solution.py:25
